TPU v7x, 32 devices: a whole 2x2x4 slice. The times are simulated.
32 devices in a mesh: rows: 4 (over z), ty: 4 (over x, core), tx: 2 (over y).
Axes of the slice: x: 2, y: 2, z: 4, core: 2. Of those that a mesh axis runs over, the one named last changes fastest.
Arguments:
- latent: bfloat16 [12, 32, 32, 16], P('rows', 'ty', 'tx'), may hold values from -6 to 6
- skip_input: bfloat16 [12, 32, 32, 768], P('rows', 'ty', 'tx'), may hold values from -6 to 6
- segment_ids: int32 [12, 32, 32], P('rows'), may hold values from 0 to 2, as said below
- embed_weight: bfloat16 [768, 16], replicated, may hold values from -1.5 to 1.5
- embed_bias: bfloat16 [768], replicated, may hold values from -1.75 to 1.75
- skip_weight: bfloat16 [1536, 768], replicated, may hold values from -0.15625 to 0.15625
- skip_bias: bfloat16 [768], replicated, may hold values from -1.75 to 1.75
- norm1_gain: bfloat16 [768], replicated, may hold values from 0.5 to 1.5
- norm1_bias: bfloat16 [768], replicated, may hold values from -1.75 to 1.75
- qkv_weight: bfloat16 [768, 2304], replicated, may hold values from -0.21875 to 0.21875
- proj_weight: bfloat16 [768, 768], replicated, may hold values from -0.875 to 0.875
- proj_bias: bfloat16 [768], replicated, may hold values from -1.75 to 1.75
- norm2_gain: bfloat16 [768], replicated, may hold values from 0.5 to 1.5
- norm2_bias: bfloat16 [768], replicated, may hold values from -1.75 to 1.75
- fc1_weight: bfloat16 [768, 3072], replicated, may hold values from -0.21875 to 0.21875
- fc1_bias: bfloat16 [3072], replicated, may hold values from -1.75 to 1.75
- fc2_weight: bfloat16 [3072, 768], replicated, may hold values from -0.109375 to 0.109375
- fc2_bias: bfloat16 [768], replicated, may hold values from -1.75 to 1.75
- conv_weight: bfloat16 [768, 144], replicated, may hold values from -0.125 to 0.125
- cotangent: bfloat16 [12, 32, 32, 16], P('rows', 'ty', 'tx'), may hold values from -6 to 6
Outputs:
- output: bfloat16 [12, 32, 32, 16], P('rows', 'ty', 'tx')
- skip_input_grad: bfloat16 [12, 32, 32, 768], P('rows', 'ty', 'tx')
- embed_weight_grad: float32 [768, 16], P('rows')
- embed_bias_grad: float32 [768], P('rows')
- skip_weight_grad: float32 [1536, 768], P('rows')
- skip_bias_grad: float32 [768], P('rows')
- norm1_gain_grad: float32 [768], P('rows')
- norm1_bias_grad: float32 [768], P('rows')
- qkv_weight_grad: float32 [768, 2304], P('rows')
- proj_weight_grad: float32 [768, 768], P('rows')
- proj_bias_grad: float32 [768], P('rows')
- norm2_gain_grad: float32 [768], P('rows')
- norm2_bias_grad: float32 [768], P('rows')
- fc1_weight_grad: float32 [768, 3072], P('rows')
- fc1_bias_grad: float32 [3072], P('rows')
- fc2_weight_grad: float32 [3072, 768], P('rows')
- fc2_bias_grad: float32 [768], P('rows')
- conv_weight_grad: float32 [768, 144], P('rows')
Inputs may be any that keep to these rules, and one draw needn't show every extreme that they name: `segment_ids`: each row's 32 x 32 grid is cut into three rectangular images: id 0 fills every grid row up to a left width, ids 1 and 2 fill the remaining columns above and below a top height; the width and the height are drawn for each row among the multiples of 4 from 8 to 24.
All inputs are finite; a program needn't handle non-finite values.
Results may differ from a plain program's by a relative error of at most 0.014.
Values may be sent and summed in bfloat16 or wider, within the bound.
A program may use at most 256 MiB of HBM per device.

v0:
```python
import functools

import jax
import jax.numpy as jnp
from jax import lax
from jax.experimental import pallas as pl
from jax.experimental.pallas import tpu as pltpu
from jax.sharding import PartitionSpec as P

MESH = pl.DeviceIdType.MESH
norm_eps = 1e-05
full_vmem = 62 * 1024 * 1024


def cell_of(token, tile, tile_height, tile_width, columns):
    down = tile // columns * tile_height + token // tile_width
    across = tile % columns * tile_width + token % tile_width
    return down, across


def fill_shift(shift_ref, tile_height, tile_width):
    tokens = tile_height * tile_width
    bands, columns = lax.axis_size("ty"), lax.axis_size("tx")
    own = lax.axis_index("ty") * columns + lax.axis_index("tx")
    lane = lax.broadcasted_iota(jnp.int32, (8, tokens), 1)
    down, across = cell_of(lane, own, tile_height, tile_width, columns)
    step = lax.broadcasted_iota(jnp.int32, (shift_ref.shape[0], tokens), 0)
    for p in range(9):
        i, j = down - (p // 3 - 1), across - (p % 3 - 1)
        inside = (i >= 0) & (i < bands * tile_height) & (j >= 0) & (j < columns * tile_width)
        tile = i // tile_height * columns + j // tile_width
        place = tile * tokens + i % tile_height * tile_width + j % tile_width
        place = jnp.where(inside, place, -1)[0:1]
        chosen = jnp.where(step == place, 1.0, 0.0)
        shift_ref[:, p * tokens : (p + 1) * tokens] = chosen.astype(jnp.bfloat16)


def same_image(cuts_ref, row, p, tile_height, tile_width):
    tokens = tile_height * tile_width
    columns = lax.axis_size("tx")
    own = lax.axis_index("ty") * columns + lax.axis_index("tx")
    lane = lax.broadcasted_iota(jnp.int32, (8, tokens), 1)
    down, across = cell_of(lane, own, tile_height, tile_width, columns)
    left_width, top_height = cuts_ref[row, 0], cuts_ref[row, 1]

    def image_of(i, j):
        return jnp.where(j < left_width, 0, jnp.where(i < top_height, 1, 2))

    there = image_of(down - (p // 3 - 1), across - (p % 3 - 1))
    return jnp.where(image_of(down, across) == there, 1.0, 0.0)[0:1]


def mm(former, latter, axis_former, axis_latter):
    return lax.dot_general(
        former,
        latter,
        (((axis_former,), (axis_latter,)), ((), ())),
        preferred_element_type=jnp.float32,
    )


def normalised(values):
    average = jnp.mean(values, axis=1, keepdims=True)
    centred = values - average
    rate = lax.rsqrt(jnp.mean(centred * centred, axis=1, keepdims=True) + norm_eps)
    return centred * rate, rate


def norm_back(incoming, unit, rate, gain):
    scaled = incoming * gain
    first = jnp.mean(scaled, axis=1, keepdims=True)
    second = jnp.mean(scaled * unit, axis=1, keepdims=True)
    return (scaled - first - unit * second) * rate


def down_sum(values):
    return jnp.sum(values, axis=0, keepdims=True)


def front_kernel(
    segment_ids, latent, cotangent, embed_turned, *refs
):
    biases, fc1_bias, refs = refs[:8], refs[8], refs[9:]
    skip_in, skip_weight_in, qkv_in, embedded, stream, normed, query, pairs, cot, vectors, hidden_bias, cuts = refs[:12]
    skip, skip_weight, qkv_weight, load_sem = refs[12:]
    sources, targets = (skip_weight_in, skip_in, qkv_in), (skip_weight, skip, qkv_weight)
    loads = [pltpu.make_async_copy(a, b, load_sem.at[k]) for k, (a, b) in enumerate(zip(sources, targets))]
    for load in loads:
        load.start()
    for k, bias in enumerate(biases):
        vectors[k : k + 1] = bias[...].reshape(1, bias.shape[0]).astype(jnp.float32)
    line = fc1_bias[...].reshape(1, fc1_bias.shape[0]).astype(jnp.float32)
    block = hidden_bias.shape[2]
    for k in range(hidden_bias.shape[0]):
        hidden_bias[k] = line[:, k * block : (k + 1) * block]
    width = skip.shape[1]
    row_count, tokens = query.shape[1], query.shape[2]
    side = segment_ids.shape[1]
    for row in range(row_count):

        def count(k, carry):
            left, top = carry
            left = left + jnp.where(segment_ids[row, 0, k] == 0, 1, 0)
            top = top + jnp.where(segment_ids[row, k, side - 1] == 1, 1, 0)
            return left, top

        left, top = lax.fori_loop(0, side, count, (jnp.int32(0), jnp.int32(0)), unroll=8)
        cuts[row, 0] = left
        cuts[row, 1] = top
        at = slice(row * tokens, (row + 1) * tokens)
        cot[row] = jnp.transpose(cotangent[at, :].astype(jnp.float32)).astype(jnp.bfloat16)
        embedded[at, :] = (mm(latent[at, :], embed_turned[...], 1, 0) + vectors[0:1]).astype(jnp.bfloat16)
    loads[0].wait()
    loads[1].wait()
    total = mm(embedded[...], skip_weight[:width], 1, 0) + mm(skip[...], skip_weight[width:], 1, 0) + vectors[1:2]
    stream[...] = total
    unit, rate = normalised(total)
    normed[...] = (unit * vectors[2:3] + vectors[3:4]).astype(jnp.bfloat16)
    loads[2].wait()
    half = width // 2
    for k in range(3):
        piece = mm(normed[...], qkv_weight[:, k * width : (k + 1) * width], 1, 0).astype(jnp.bfloat16)
        for g in range(2):
            part = piece[:, g * half : (g + 1) * half].reshape(row_count, tokens, half)
            if k == 0:
                query[g] = part
            else:
                pairs[g, :, :, (k - 1) * half : k * half] = part


def front(segment_ids, latent, cotangent, embed_turned, biases, fc1_bias, skip, skip_weight, qkv_weight, row_count):
    token_count, width = skip.shape
    tokens = token_count // row_count
    low, wide = jnp.bfloat16, jnp.float32
    smem, vmem = pl.BlockSpec(memory_space=pltpu.SMEM), pl.BlockSpec(memory_space=pltpu.VMEM)
    return pl.pallas_call(
        front_kernel,
        out_shape=[
            jax.ShapeDtypeStruct((token_count, width), low),
            jax.ShapeDtypeStruct((token_count, width), wide),
            jax.ShapeDtypeStruct((token_count, width), low),
            jax.ShapeDtypeStruct((2, row_count, tokens, width // 2), low),
            jax.ShapeDtypeStruct((2, row_count, tokens, width), low),
            jax.ShapeDtypeStruct((row_count, cotangent.shape[1], tokens), low),
            jax.ShapeDtypeStruct((8, width), wide),
            jax.ShapeDtypeStruct((fc1_bias.shape[0] // width, 1, width), wide),
            jax.ShapeDtypeStruct((row_count, 2), jnp.int32),
        ],
        in_specs=[smem] + [vmem] * 12 + [pl.BlockSpec(memory_space=pl.ANY)] * 3,
        out_specs=[vmem] * 8 + [smem],
        scratch_shapes=[pltpu.VMEM(entry.shape, low) for entry in (skip, skip_weight, qkv_weight)]
        + [pltpu.SemaphoreType.DMA((3,))],
        compiler_params=pltpu.CompilerParams(vmem_limit_bytes=full_vmem),
        name="front",
    )(segment_ids, latent, cotangent, embed_turned, *biases, fc1_bias, skip, skip_weight, qkv_weight)


def erf_of(values):
    x = jnp.clip(values, -4.0, 4.0)
    square = x * x
    upper = square * -2.72614225801306e-10 + 2.77068142495902e-08
    for term in (-2.10102402082508e-06, -5.69250639462346e-05, -7.34990630326855e-04, -2.95459980854025e-03, -1.60960333262415e-02):
        upper = upper * square + term
    lower = square * -1.45660718464996e-05 + -2.13374055278905e-04
    for term in (-1.68282697438203e-03, -7.37332916720468e-03, -1.42647390514189e-02):
        lower = lower * square + term
    return x * upper / lower


def middle_kernel(
    paired, attended, stream, out_grad, proj_weight, vectors, hidden_bias, active_grad, fc1_weight, fc2_weight,
    fc1_out, fc2_out, hidden_bias_grad, proj_grad, attended_grad, mid_grad, conv_in, vector_grads,
    middle, normed, out_low, forward_sum, backward_sum, grad1, grad2, *refs
):
    step = pl.program_id(0)
    last = fc2_out.shape[0] // fc2_weight.shape[0] - 1
    token_count, width = stream.shape
    block = fc1_weight.shape[1]
    low = jnp.bfloat16
    parts = [slice(0, token_count)]
    store_sem = refs[-1]
    if paired:
        got1, got2, total1, total2, send_sem, recv_sem = refs[:6]
        z, ty, y = lax.axis_index("rows"), lax.axis_index("ty"), lax.axis_index("tx")
        core = lax.rem(ty, 2)
        peer = (z, ty + 1 - 2 * core, y)

    def stores(k):
        slot = lax.rem(k, 2)
        first, second = (total1, total2) if paired else (grad1, grad2)
        across = first.shape[3]
        down = second.shape[1]
        return [
            pltpu.make_async_copy(
                first.at[slot], fc1_out.at[:, :, pl.ds(pl.multiple_of(k * across, 128), across)], store_sem.at[slot, 0]
            ),
            pltpu.make_async_copy(
                second.at[slot], fc2_out.at[pl.ds(pl.multiple_of(k * down, 16), down)], store_sem.at[slot, 1]
            ),
        ]

    def swaps(k):
        slot = lax.rem(k, 2)
        theirs1 = pl.ds(pl.multiple_of((1 - core) * (block // 2), 128), block // 2)
        theirs2 = pl.ds(pl.multiple_of((1 - core) * (width // 2), 128), width // 2)
        pairs = ((grad1.at[slot, :, :, theirs1], got1.at[k]), (grad2.at[slot, :, theirs2], got2.at[k]))
        return [
            pltpu.make_async_remote_copy(
                src_ref=source,
                dst_ref=target,
                send_sem=send_sem.at[k, n],
                recv_sem=recv_sem.at[k, n],
                device_id=peer,
                device_id_type=MESH,
            )
            for n, (source, target) in enumerate(pairs)
        ]

    def settle(k):
        slot = lax.rem(k, 2)
        if paired:
            for copy in swaps(k):
                copy.wait()

            @pl.when(k >= 2)
            def _():
                for copy in stores(k - 2):
                    copy.wait()

            mine1 = pl.ds(pl.multiple_of(core * (block // 2), 128), block // 2)
            mine2 = pl.ds(pl.multiple_of(core * (width // 2), 128), width // 2)
            total1[slot] = grad1[slot, :, :, mine1] + got1[k]
            total2[slot] = grad2[slot, :, mine2] + got2[k]
        for copy in stores(k):
            copy.start()

    @pl.when(step == 0)
    def _():
        if paired:
            greet([peer])
        total = jnp.zeros((1, width), jnp.float32)
        for at in parts:
            grad = out_grad[at, :]
            out_low[at, :] = grad.astype(low)
            total = total + down_sum(grad)
            value = stream[at, :] + vectors[4:5]
            for k in range(2):
                value = value + mm(attended[k], proj_weight[k * width // 2 : (k + 1) * width // 2], 1, 0)
            middle[at, :] = value
            unit, rate = normalised(value)
            normed[at, :] = (unit * vectors[5:6] + vectors[6:7]).astype(low)
        vector_grads[7:8] = total
        forward_sum[...] = jnp.zeros_like(forward_sum)
        backward_sum[...] = jnp.zeros_like(backward_sum)

    slot = lax.rem(step, 2)
    if not paired:

        @pl.when(step >= 2)
        def _():
            for copy in stores(step - 2):
                copy.wait()

    bias_grad = jnp.zeros((1, block), jnp.float32)
    actives, hidden_lows = [], []
    for at in parts:
        hidden = mm(normed[at, :], fc1_weight[...], 1, 0) + hidden_bias[0]
        share = 0.5 + 0.5 * erf_of(hidden * 0.7071067811865476)
        density = jnp.exp(hidden * hidden * -0.5) * 0.3989422804014327
        active = (hidden * share).astype(low)
        hidden_grad = active_grad[at, :].astype(jnp.float32) * (share + hidden * density)
        bias_grad = bias_grad + down_sum(hidden_grad)
        hidden_low = hidden_grad.astype(low)
        forward_sum[at, :] = forward_sum[at, :] + mm(active, fc2_weight[...], 1, 0)
        backward_sum[at, :] = backward_sum[at, :] + mm(hidden_low, fc1_weight[...], 1, 1)
        actives.append(active)
        hidden_lows.append(hidden_low)
    hidden_bias_grad[0] = bias_grad
    grad2[slot] = mm(jnp.concatenate(actives, axis=0), out_low[...], 0, 0).astype(low)
    grad1[slot] = mm(normed[...], jnp.concatenate(hidden_lows, axis=0), 0, 0).astype(low).reshape(grad1.shape[1:])
    if paired:
        for copy in swaps(step):
            copy.start()

        @pl.when(step > 0)
        def _():
            settle(step - 1)
    else:
        settle(step)

    @pl.when(step == last)
    def _():
        gain_sum = jnp.zeros((1, width), jnp.float32)
        bias_sum = jnp.zeros((1, width), jnp.float32)
        mid_sum = jnp.zeros((1, width), jnp.float32)
        lows = []
        for at in parts:
            unit, rate = normalised(middle[at, :])
            conv_in[at, :] = (middle[at, :] + forward_sum[at, :] + vectors[7:8]).astype(low)
            incoming = backward_sum[at, :]
            gain_sum = gain_sum + down_sum(incoming * unit)
            bias_sum = bias_sum + down_sum(incoming)
            grad = out_grad[at, :] + norm_back(incoming, unit, rate, vectors[5:6])
            mid_grad[at, :] = grad
            mid_sum = mid_sum + down_sum(grad)
            mid_low = grad.astype(low)
            lows.append(mid_low)
            for k in range(2):
                attended_grad[k] = mm(mid_low, proj_weight[k * width // 2 : (k + 1) * width // 2], 1, 1).astype(low)
        for k in range(2):
            proj_grad[k * width // 2 : (k + 1) * width // 2] = mm(attended[k], lows[0], 0, 0).astype(low)
        vector_grads[4:5] = mid_sum
        vector_grads[5:6] = gain_sum
        vector_grads[6:7] = bias_sum
        if paired:
            settle(step)
        for k in (last - 1, last):
            for copy in stores(k):
                copy.wait()


def middle(attended, stream, out_grad, active_grad, proj_weight, vectors, hidden_bias, fc1_weight, fc2_weight, paired):
    token_count, width = stream.shape
    hidden_width = fc1_weight.shape[1]
    steps, _, block = hidden_bias.shape
    low, wide = jnp.bfloat16, jnp.float32
    cut = 2 if paired else 1
    vmem, anywhere = pl.BlockSpec(memory_space=pltpu.VMEM), pl.BlockSpec(memory_space=pl.ANY)
    scratch = [
        pltpu.VMEM((token_count, width), wide),
        pltpu.VMEM((token_count, width), low),
        pltpu.VMEM((token_count, width), low),
        pltpu.VMEM((token_count, width), wide),
        pltpu.VMEM((token_count, width), wide),
        pltpu.VMEM((2, 4, width // 4, block), low),
        pltpu.VMEM((2, block, width), low),
    ]
    if paired:
        scratch += [
            pltpu.VMEM((steps, 4, width // 4, block // 2), low),
            pltpu.VMEM((steps, block, width // 2), low),
            pltpu.VMEM((2, 4, width // 4, block // 2), low),
            pltpu.VMEM((2, block, width // 2), low),
            pltpu.SemaphoreType.DMA((steps, 2)),
            pltpu.SemaphoreType.DMA((steps, 2)),
        ]
        params = pltpu.CompilerParams(collective_id=4, has_side_effects=True, vmem_limit_bytes=full_vmem)
    else:
        params = pltpu.CompilerParams(vmem_limit_bytes=full_vmem)
    return pl.pallas_call(
        functools.partial(middle_kernel, paired),
        grid=(steps,),
        out_shape=[
            jax.ShapeDtypeStruct((4, width // 4, hidden_width // cut), low),
            jax.ShapeDtypeStruct((hidden_width, width // cut), low),
            jax.ShapeDtypeStruct((steps, 1, block), wide),
            jax.ShapeDtypeStruct((width, width), low),
            jax.ShapeDtypeStruct((2, token_count, width // 2), low),
            jax.ShapeDtypeStruct((token_count, width), wide),
            jax.ShapeDtypeStruct((token_count, width), low),
            jax.ShapeDtypeStruct((8, width), wide),
        ],
        in_specs=[vmem] * 5
        + [
            pl.BlockSpec((1, 1, block), lambda k: (k, 0, 0)),
            pl.BlockSpec((token_count, block), lambda k: (0, k)),
            pl.BlockSpec((width, block), lambda k: (0, k)),
            pl.BlockSpec((block, width), lambda k: (k, 0)),
        ],
        out_specs=[anywhere, anywhere, pl.BlockSpec((1, 1, block), lambda k: (k, 0, 0))] + [vmem] * 5,
        scratch_shapes=scratch + [pltpu.SemaphoreType.DMA((2, 2))],
        compiler_params=params,
        name="middle",
    )(attended, stream, out_grad, proj_weight, vectors, hidden_bias, active_grad, fc1_weight, fc2_weight)


rear_order = (
    "+proj", "+fc2b", "+fc2a", "grad0", "grad1", "grad2", "+qkv0", "+qkv2", "norm", "+qkv0", "+qkv1", "skip",
    "+qkv0", "+qkv2", "+skip", "joined", "+qkv2", "+thin", "+proj", "+qkv1", "+skip", "+thin", "+qkv1", "+fc1",
    "=qkv0", "+fc2b", "+proj", "+skip", "+flat", "+thin", "+fc2a", "=qkv1", "=qkv2", "+qkv0", "+fc1", "+qkv1",
    "+fc2a", "+flat", "+fc2b", "+qkv2", "=skip", "+qkv1", "+fc2a", "+proj", "+fc2b", "+flat", "+qkv0", "+fc1",
    "input", "+qkv0", "=thin", "=flat", "+fc1", "+qkv1", "+qkv2", "+skip", "+fc2a", "+thin", "+flat", "+qkv2",
    "+fc2a", "+flat", "+skip", "+thin",
)


def rear_kernel(
    kinds, reduces, projected_in, qkv_in, normed_in, stream_in, mid_in, embedded_in, skip_in, skip_weight_in,
    latent, vectors, middle_grads, hidden_bias_grad, conv_grad, *refs
):
    count = len(kinds)
    resumed, refs = refs[:count], refs[count:]
    skip_input_grad, refs = refs[0], refs[1:]
    if reduces:
        sums, refs = refs[: count + 6], refs[count + 6 :]
        peers = chip_peers()
    grads, refs = refs[:6], refs[6:]
    skip_grad, thin, flat = grads[3:]
    projected_grad, qkv_weight, normed, stream, mid_grad, embedded, skip, skip_weight, stream_low, load_sem = refs[:10]
    sources = (projected_in, normed_in, qkv_in, stream_in, mid_in, embedded_in, skip_in, skip_weight_in)
    targets = (projected_grad, normed, qkv_weight, stream, mid_grad, embedded, skip, skip_weight)
    loads = [pltpu.make_async_copy(a, b, load_sem.at[k]) for k, (a, b) in enumerate(zip(sources, targets))]
    for load in loads[:3]:
        load.start()
    named = {}
    if reduces:
        items = make_reducers(kinds + (("plane", False),) * 6, resumed + grads, sums, refs[10:], range(count + 3))
        named = dict(zip(("fc1", "fc2a", "fc2b", "proj", "qkv0", "qkv1", "qkv2", "skip", "thin", "flat"), items))
        greet([peers[name] for name in ("core", "x", "y", "xy")] + peers["z"])
        for item in items[:count]:
            item.begin()
    for load in loads[3:]:
        load.start()
    width = stream.shape[1]
    low = jnp.bfloat16
    made = {}

    def open_up(*names):
        for name in names:
            if reduces:
                named[name].begin()

    def weight_grad(k):
        if k == 0:
            loads[0].wait()
            loads[1].wait()
        piece = mm(normed[...], projected_grad[:, k * width : (k + 1) * width], 0, 0)
        grads[k][...] = piece.astype(low).reshape(grads[k].shape)
        open_up(f"qkv{k}")

    def norm():
        for load in loads[2:5]:
            load.wait()
        incoming = mm(projected_grad[...], qkv_weight[...], 1, 1)
        unit, rate = normalised(stream[...])
        grad = mid_grad[...] + norm_back(incoming, unit, rate, vectors[2:3])
        made["rows"] = [down_sum(grad), down_sum(incoming * unit), down_sum(incoming)]
        stream_low[...] = grad.astype(low)

    def skip_weight_grad():
        loads[5].wait()
        loads[6].wait()
        skip_grad[0:2] = mm(embedded[...], stream_low[...], 0, 0).astype(low).reshape(2, width // 2, width)
        skip_grad[2:4] = mm(skip[...], stream_low[...], 0, 0).astype(low).reshape(2, width // 2, width)
        open_up("skip")

    def joined():
        loads[7].wait()
        embed_grad = mm(stream_low[...], skip_weight[:width], 1, 1)
        embed_weight_grad = mm(embed_grad.astype(low), latent[...], 0, 0)
        rest = jnp.zeros((width, 128 - 2 * 16), jnp.float32)
        thin[:, :, :128] = conv_grad[:, :128].astype(low).reshape(4, width // 4, 128)
        edge = jnp.concatenate([conv_grad[:, 128:144], embed_weight_grad, rest], axis=1)
        thin[:, :, 128:] = edge.astype(low).reshape(4, width // 4, 128)
        rows = [down_sum(embed_grad)] + made["rows"] + [middle_grads[k : k + 1] for k in range(4, 8)]
        stack = jnp.concatenate(rows, axis=0)
        share = width // 4
        hidden_line = jnp.concatenate([hidden_bias_grad[k] for k in range(hidden_bias_grad.shape[0])], axis=1)
        for block in range(4):
            own = stack[:, block * share : (block + 1) * share]
            own = jnp.concatenate([own, jnp.zeros((8, 256 - share), jnp.float32)], axis=1)
            line = hidden_line[:, block * width : (block + 1) * width]
            pieces = [line[:, k * 256 : (k + 1) * 256] for k in range(width // 256)]
            body = jnp.concatenate([own] + pieces + [jnp.zeros((8 - len(pieces), 256), jnp.float32)], axis=0)
            flat[block, 0:16] = body.astype(low)
            flat[block, 16:64] = jnp.zeros((48, 256), low)
        open_up("thin", "flat")

    def input_grad():
        skip_input_grad[...] = mm(stream_low[...], skip_weight[width:], 1, 1).astype(low)

    acts = {"norm": norm, "skip": skip_weight_grad, "joined": joined, "input": input_grad}
    for entry in rear_order:
        if entry[0] in "+=":
            if reduces:
                named[entry[1:]].step()
                if entry[0] == "=":
                    named[entry[1:]].step()
        elif entry[:-1] == "grad":
            weight_grad(int(entry[-1]))
        else:
            acts[entry]()
    assert not any(item.stages for item in named.values())


def rear(projected_grad, qkv_weight, normed, stream, mid_grad, embedded, skip, skip_weight, latent, vectors, middle_grads, hidden_bias_grad, conv_grad, resumed, reduces):
    token_count, width = stream.shape
    low = jnp.bfloat16
    kinds = tuple((start, True) for start, _, _ in resumed)
    sizes = [(width // 4, width)] * 3 + [(width // 2, width), (width // 4, 256), (64, 256)]
    totals = [shape for _, _, shape in resumed] + [(r, c // 2) for r, c in sizes]
    vmem, anywhere = pl.BlockSpec(memory_space=pltpu.VMEM), pl.BlockSpec(memory_space=pl.ANY)
    big = [projected_grad, qkv_weight, normed, stream, mid_grad, embedded, skip, skip_weight]
    out_shape = [jax.ShapeDtypeStruct((token_count, width), low)]
    out_specs = [vmem]
    scratch = []
    if reduces:
        out_shape += [jax.ShapeDtypeStruct((2,) + shape, low) for shape in totals]
        out_specs += [anywhere] * len(totals)
        scratch += [pltpu.VMEM((4,) + shape, low) for shape in sizes]
        params = pltpu.CompilerParams(collective_id=3, has_side_effects=True, vmem_limit_bytes=full_vmem)
    else:
        out_shape += [jax.ShapeDtypeStruct((4,) + shape, low) for shape in sizes]
        out_specs += [vmem] * len(sizes)
        params = pltpu.CompilerParams(vmem_limit_bytes=full_vmem)
    scratch += [pltpu.VMEM(entry.shape, entry.dtype) for entry in big]
    scratch += [pltpu.VMEM((token_count, width), low), pltpu.SemaphoreType.DMA((len(big),))]
    if reduces:
        scratch += reducer_scratch(kinds + (("plane", False),) * 6, totals)
    return pl.pallas_call(
        functools.partial(rear_kernel, kinds, reduces),
        out_shape=out_shape,
        in_specs=[anywhere] * len(big) + [vmem] * 5 + [anywhere] * len(kinds),
        out_specs=out_specs,
        scratch_shapes=scratch,
        compiler_params=params,
        name="rear",
    )(*big, latent, vectors, middle_grads, hidden_bias_grad, conv_grad, *[entry for _, entry, _ in resumed])


def finish_kernel(patch, plan, *refs):
    count = len(plan)
    sums, (thin, flat, conv_out) = refs[:count], refs[count : count + 3]
    totals, refs = refs[count + 3 : count + 8], refs[count + 8 :]
    (embed_turned, conv_turned), lines, fc1_line, output, refs = refs[:2], refs[2:10], refs[10], refs[11], refs[12:]
    lows, wides, load_sem, store_sem = refs[:count], refs[count : count + 5], refs[count + 5], refs[count + 6]
    loads = [pltpu.make_async_copy(a, b, load_sem.at[k]) for k, (a, b) in enumerate(zip(sums, lows))]
    for load in loads:
        load.start()
    stores = []
    for k, (low, (which, start, piece, left)) in enumerate(zip(lows, plan)):
        loads[k].wait()
        wide = wides[which]
        half, depth = low.shape[2], low.shape[1]

        def body(i, carry):
            at = pl.ds(pl.multiple_of(i * 16, 16), 16)
            to = pl.ds(pl.multiple_of(start + i * 16, 16), 16)
            for core in range(2):
                for n in range(half // piece):
                    column = left + (2 * n + core) * piece
                    wide[to, column : column + piece] = low[core, at, n * piece : (n + 1) * piece].astype(jnp.float32)
            return carry

        lax.fori_loop(0, depth // 16, body, 0)
        there = (pl.ds(start, depth), pl.ds(left, 2 * half))
        store = pltpu.make_async_copy(wide.at[there], totals[which].at[there], store_sem.at[k])
        store.start()
        stores.append(store)
    share = thin.shape[1]
    turned = jnp.transpose(jnp.concatenate([thin[0], thin[1]], axis=1).astype(jnp.float32))
    taps = 9 * patch
    conv_turned[...] = turned[:taps]
    embed_turned[...] = turned[taps : taps + patch]
    rows = jnp.concatenate([flat[0, 0:16, :], flat[1, 0:16, :]], axis=1).astype(jnp.float32)
    for k, line in enumerate(lines):
        line[...] = rows[k : k + 1, :share].reshape(share)
    fc1_line[...] = jnp.concatenate([rows[k : k + 1] for k in range(8, 11)], axis=1).reshape(fc1_line.shape[0])
    for row in range(output.shape[0]):
        output[row] = jnp.transpose(conv_out[row].astype(jnp.float32)).astype(jnp.bfloat16)
    for store in stores:
        store.wait()


def finish(sums, thin, flat, conv_out):
    row_count, patch, tokens = conv_out.shape
    share = thin.shape[1]
    wide = jnp.float32
    plan = tuple(entry[:4] for entry in sums)
    arrays = [entry[4] for entry in sums]
    whole = [(0, 0)] * 5
    for which, start, _, left, entry in sums:
        rows, columns = whole[which]
        whole[which] = (max(rows, start + entry.shape[1]), max(columns, left + 2 * entry.shape[2]))
    vmem, anywhere = pl.BlockSpec(memory_space=pltpu.VMEM), pl.BlockSpec(memory_space=pl.ANY)
    return pl.pallas_call(
        functools.partial(finish_kernel, patch, plan),
        out_shape=[jax.ShapeDtypeStruct(shape, wide) for shape in whole]
        + [jax.ShapeDtypeStruct((patch, share), wide), jax.ShapeDtypeStruct((9 * patch, share), wide)]
        + [jax.ShapeDtypeStruct((share,), wide)] * 8
        + [jax.ShapeDtypeStruct((4 * share,), wide), jax.ShapeDtypeStruct((row_count, tokens, patch), jnp.bfloat16)],
        in_specs=[anywhere] * len(arrays) + [vmem] * 3,
        out_specs=[anywhere] * 5 + [vmem] * 12,
        scratch_shapes=[pltpu.VMEM(entry.shape, jnp.bfloat16) for entry in arrays]
        + [pltpu.VMEM(shape, wide) for shape in whole]
        + [pltpu.SemaphoreType.DMA((len(arrays),)), pltpu.SemaphoreType.DMA((len(arrays),))],
        compiler_params=pltpu.CompilerParams(vmem_limit_bytes=full_vmem),
        name="finish",
    )(*arrays, thin, flat, conv_out)


def plane_peers():
    z, ty, y = lax.axis_index("rows"), lax.axis_index("ty"), lax.axis_index("tx")
    core, x = lax.rem(ty, 2), ty // 2
    here = x * 2 + core
    across = (1 - x) * 2 + core
    tiles = {
        "own": here * 2 + y,
        "x": across * 2 + y,
        "y": here * 2 + 1 - y,
        "xy": across * 2 + 1 - y,
    }
    peers = {
        "core": (z, x * 2 + 1 - core, y),
        "x": (z, across, y),
        "y": (z, here, 1 - y),
    }
    return tiles, peers


def plane_peer(k):
    z, ty, y = lax.axis_index("rows"), lax.axis_index("ty"), lax.axis_index("tx")
    x, core = ty // 2, lax.rem(ty, 2)
    flip_x, flip_core, flip_y = k // 4, k // 2 % 2, k % 2
    x = x + flip_x - 2 * flip_x * x
    core = core + flip_core - 2 * flip_core * core
    y = y + flip_y - 2 * flip_y * y
    return (z, x * 2 + core, y), (x * 2 + core) * 2 + y


def greet(peers):
    barrier = pltpu.get_barrier_semaphore()
    for peer in peers:
        pl.semaphore_signal(barrier, inc=1, device_id=peer, device_id_type=MESH)
    pl.semaphore_wait(barrier, len(peers))


def fill_mask(mask_ref, cuts_ref, row, tile, tile_height, tile_width):
    columns = lax.axis_size("tx")
    tokens = tile_height * tile_width
    left_width = cuts_ref[row, 0]
    top_height = cuts_ref[row, 1]

    def image_of(down, across):
        return jnp.where(across < left_width, 0, jnp.where(down < top_height, 1, 2))

    lane = lax.broadcasted_iota(jnp.int32, (8, tokens), 1)
    mine = image_of(*cell_of(lane, tile, tile_height, tile_width, columns))[0:1]
    step = lax.broadcasted_iota(jnp.int32, (tokens, tokens), 0)
    down, across = step // tile_width, step % tile_width
    for other in range(mask_ref.shape[0] // tokens):
        theirs = image_of(
            down + other // columns * tile_height, across + other % columns * tile_width
        )
        mask_ref[other * tokens : (other + 1) * tokens, :] = jnp.where(mine == theirs, 0.0, -1e30)


def two_heads(pair, scale):
    lane = lax.broadcasted_iota(jnp.int32, pair.shape, 1)
    wide = pair.astype(jnp.float32) * scale
    first = jnp.where(lane < pair.shape[1] // 2, wide, 0.0)
    return jnp.concatenate([first, wide - first], axis=0).astype(jnp.bfloat16)


def own_blocks(both):
    head, tokens = both.shape[0] // 2, both.shape[1] // 2
    return jnp.concatenate([both[:head, :tokens], both[head:, tokens:]], axis=0)


def attend_kernel(
    tile_height, tile_width, cuts, query, pairs, cot, conv_turned, fc2_in,
    out, lse, query_out, attended_out, all_out, spread, out_grad_out, active_grad_out,
    cot_all, queries, held, results, scores, mask, shift, fc2_weight, out_grad, active_grad,
    local_sem, send_sem, recv_sem, cot_sem, cot_send_sem, cot_recv_sem, side_sem
):
    _, row_count, tokens, half = query.shape
    tile_count = held.shape[1]
    width = 2 * half
    tiles, peers = plane_peers()
    own = tiles["own"]
    x = lax.axis_index("ty") // 2
    fc2_load = pltpu.make_async_copy(fc2_in, fc2_weight, side_sem.at[0])
    fc2_load.start()
    greet([plane_peer(k)[0] for k in range(1, tile_count)])
    cot_copies = [pltpu.make_async_copy(cot, cot_all.at[own], cot_sem.at[0])]
    for k in range(1, tile_count):
        cot_copies.append(
            pltpu.make_async_remote_copy(
                src_ref=cot,
                dst_ref=cot_all.at[own],
                send_sem=cot_send_sem.at[k],
                recv_sem=cot_recv_sem.at[k],
                device_id=plane_peer(k)[0],
                device_id_type=MESH,
            )
        )

    def send(row, slot, source, target, peer):
        copy = pltpu.make_async_remote_copy(
            src_ref=source,
            dst_ref=target,
            send_sem=send_sem.at[row, slot],
            recv_sem=recv_sem.at[row, slot],
            device_id=peer,
            device_id_type=MESH,
        )
        copy.start()
        flights[row][slot] = copy

    def keep(row, slot, source, target):
        copy = pltpu.make_async_copy(source, target, local_sem.at[row, slot])
        copy.start()
        kept[row][slot] = copy

    flights = [{} for _ in range(row_count)]
    kept = [{} for _ in range(row_count)]

    def begin(row):
        here = held.at[row, own]
        send(row, 1, pairs.at[1 - x, row], here, peers["x"])
        send(row, 0, query.at[1 - x, row], queries.at[row, 1], peers["x"])
        send(row, 2, pairs.at[x, row], here, peers["y"])
        send(row, 3, pairs.at[x, row], here, peers["core"])
        keep(row, 0, query.at[x, row], queries.at[row, 0])
        keep(row, 1, pairs.at[x, row], here)

    def forward(row):
        flights[row][1].wait_recv()
        tile = held.at[row, tiles["x"]]
        send(row, 4, tile, tile, peers["y"])
        send(row, 5, tile, tile, peers["core"])
        flights[row][2].wait_recv()
        tile = held.at[row, tiles["y"]]
        send(row, 6, tile, tile, peers["core"])

    def gather_row(row):
        flights[row][4].wait_recv()
        tile = held.at[row, tiles["xy"]]
        send(row, 7, tile, tile, peers["core"])
        for slot in (0, 3, 5, 6, 7):
            flights[row][slot].wait_recv()
        for slot in range(8):
            flights[row][slot].wait_send()
        for slot in range(2):
            kept[row][slot].wait()
        keep(row, 3, held.at[row], all_out.at[row])
        keep(row, 4, queries.at[row], query_out.at[row])

    chunk = 2

    def compute(row):
        def one_pair(p, carry, which=(0, 1)):
            at = pl.ds(pl.multiple_of(p * 128, 128), 128)
            at_value = pl.ds(pl.multiple_of(half + p * 128, 128), 128)
            for t in which:
                both = two_heads(queries[row, t, :, at], 0.125)
                peak = None
                for c in range(tile_count // chunk):
                    span = slice(c * chunk * tokens, (c + 1) * chunk * tokens)
                    keys = held[row, c * chunk : (c + 1) * chunk, :, at].reshape(chunk * tokens, 128)
                    extra = mask[row, t, span, :]
                    part = mm(keys, both, 1, 1) + jnp.concatenate([extra, extra], axis=1)
                    scores[t, span, :] = part
                    top = jnp.max(part, axis=0, keepdims=True)
                    peak = top if peak is None else jnp.maximum(peak, top)
                total = jnp.zeros_like(peak)
                summed = jnp.zeros((128, 2 * tokens), jnp.float32)
                for c in range(tile_count // chunk):
                    span = slice(c * chunk * tokens, (c + 1) * chunk * tokens)
                    values = held[row, c * chunk : (c + 1) * chunk, :, at_value].reshape(chunk * tokens, 128)
                    part = jnp.exp(scores[t, span, :] - peak)
                    total = total + jnp.sum(part, axis=0, keepdims=True)
                    summed = summed + mm(values, part.astype(jnp.bfloat16), 0, 0)
                blocks = own_blocks(summed / total)
                results[row, t, :, at] = jnp.transpose(blocks).astype(jnp.bfloat16)
                lse[row, p, t] = peak + jnp.log(total)
            return carry

        if row < row_count - 1:
            lax.fori_loop(0, half // 128, one_pair, 0)
            hand_back(row)
        else:
            lax.fori_loop(0, half // 128, functools.partial(one_pair, which=(1,)), 0)
            hand_back(row)
            lax.fori_loop(0, half // 128, functools.partial(one_pair, which=(0,)), 0)
        keep(row, 5, results.at[row, 0], out.at[x, row])
        keep(row, 6, results.at[row], attended_out.at[row])

    def hand_back(row):
        send(row, 8, results.at[row, 1], out.at[x, row], peers["x"])

    side_copies = []
    parts = [slice(k * tokens, (k + 1) * tokens) for k in range(row_count)]

    def spread_out():
        patch = cot_all.shape[2]
        turned = jnp.concatenate(
            [cot_all[t].reshape(row_count * patch, tokens) for t in range(tile_count)], axis=1
        )
        moved = mm(turned, shift[...], 1, 0)
        for row in range(row_count):
            for p in range(9):
                piece = moved[row * patch : (row + 1) * patch, p * tokens : (p + 1) * tokens]
                piece = piece * same_image(cuts, row, p, tile_height, tile_width)
                spread[p * patch : (p + 1) * patch, parts[row]] = piece.astype(jnp.bfloat16)
        out_grad[...] = mm(spread[...], conv_turned[...], 0, 0)
        copy = pltpu.make_async_copy(out_grad, out_grad_out, side_sem.at[1])
        copy.start()
        side_copies.append(copy)

    def activate():
        for k in range(fc2_weight.shape[0] // width):
            span = slice(k * width, (k + 1) * width)
            low = out_grad[...].astype(jnp.bfloat16)
            active_grad[:, span] = mm(low, fc2_weight[span, :], 1, 1).astype(jnp.bfloat16)
        copy = pltpu.make_async_copy(active_grad, active_grad_out, side_sem.at[2])
        copy.start()
        side_copies.append(copy)

    for copy in cot_copies:
        copy.start()
    begin(0)
    fill_shift(shift, tile_height, tile_width)
    for copy in cot_copies:
        copy.wait()
    spread_out()
    forward(0)
    for row in range(1, min(row_count, 3)):
        begin(row)
    fc2_load.wait()
    activate()
    for row in range(row_count):
        for t, name in enumerate(("own", "x")):
            fill_mask(mask.at[row, t], cuts, row, tiles[name], tile_height, tile_width)
    for row in range(row_count):
        gather_row(row)
        compute(row)
        for later in range(1 if row == 0 else row + 2, min(row + 3, row_count)):
            if later > 2:
                begin(later)
            forward(later)
    for row in range(row_count):
        flights[row][8].wait()
        for slot in range(3, 7):
            kept[row][slot].wait()
    for copy in side_copies:
        copy.wait()


def attend(cuts, query, pairs, cot, conv_turned, fc2_weight, tile_height, tile_width):
    _, row_count, tokens, half = query.shape
    tile_count = lax.axis_size("ty") * lax.axis_size("tx")
    width = 2 * half
    low, wide = jnp.bfloat16, jnp.float32
    vmem, anywhere = pl.BlockSpec(memory_space=pltpu.VMEM), pl.BlockSpec(memory_space=pl.ANY)
    return pl.pallas_call(
        functools.partial(attend_kernel, tile_height, tile_width),
        out_shape=[
            jax.ShapeDtypeStruct((2, row_count, tokens, half), low),
            jax.ShapeDtypeStruct((row_count, half // 128, 2, 1, 2 * tokens), wide),
            jax.ShapeDtypeStruct((row_count, 2, tokens, half), low),
            jax.ShapeDtypeStruct((row_count, 2, tokens, half), low),
            jax.ShapeDtypeStruct((row_count, tile_count, tokens, width), low),
            jax.ShapeDtypeStruct((conv_turned.shape[0], row_count * tokens), low),
            jax.ShapeDtypeStruct((row_count * tokens, width), wide),
            jax.ShapeDtypeStruct((row_count * tokens, fc2_weight.shape[0]), low),
        ],
        in_specs=[pl.BlockSpec(memory_space=pltpu.SMEM)] + [anywhere] * 3 + [vmem, anywhere],
        out_specs=[anywhere, vmem] + [anywhere] * 3 + [vmem] + [anywhere] * 2,
        scratch_shapes=[
            pltpu.VMEM((tile_count,) + cot.shape, low),
            pltpu.VMEM((row_count, 2, tokens, half), low),
            pltpu.VMEM((row_count, tile_count, tokens, width), low),
            pltpu.VMEM((row_count, 2, tokens, half), low),
            pltpu.VMEM((2, tile_count * tokens, 2 * tokens), wide),
            pltpu.VMEM((row_count, 2, tile_count * tokens, tokens), wide),
            pltpu.VMEM((tile_count * tokens, 9 * tokens), low),
            pltpu.VMEM(fc2_weight.shape, low),
            pltpu.VMEM((row_count * tokens, width), wide),
            pltpu.VMEM((row_count * tokens, fc2_weight.shape[0]), low),
            pltpu.SemaphoreType.DMA((row_count, 7)),
            pltpu.SemaphoreType.DMA((row_count, 9)),
            pltpu.SemaphoreType.DMA((row_count, 9)),
            pltpu.SemaphoreType.DMA((1,)),
            pltpu.SemaphoreType.DMA((tile_count,)),
            pltpu.SemaphoreType.DMA((tile_count,)),
            pltpu.SemaphoreType.DMA((3,)),
        ],
        compiler_params=pltpu.CompilerParams(
            collective_id=1, has_side_effects=True, vmem_limit_bytes=full_vmem
        ),
        name="attend",
    )(cuts, query, pairs, cot, conv_turned, fc2_weight)


back_order = (
    "+fc2b", "+fc1", "compute0", "+fc2a", "begin0", "scatter0", "compute1", "+fc1", "begin1", "+proj", "compute2",
    "+fc2b", "pass0", "+fc1", "+proj", "=fc2a", "begin2", "scatter1", "+fc2b", "scatter2", "convolve", "pass1",
    "+proj", "pass2", "=fc2b", "=fc1", "=proj",
)


def attend_back_kernel(
    tile_height, tile_width, kinds, cuts, query_in, attended_in, grad_in, lse_in, conv_in, conv_turned, spread,
    all_pairs, *refs
):
    count = max([kind[2] for kind in kinds], default=-1) + 1
    sources, refs = refs[:count], refs[count:]
    total_count = len(kinds)
    (out, conv_grad, conv_out), saved, refs = refs[:3], refs[3 : 3 + total_count], refs[3 + total_count :]
    query, attended, grad, lse, row_sem = refs[:5]
    held, terms, core_terms, y_terms, x_terms, x_query, query_grad, mask, shift, taps, part, part_got = refs[5:17]
    send_sem, recv_sem, part_send_sem, part_recv_sem = refs[17:21]
    grads = [
        sources[which] if rows is None else sources[which].at[:, rows[0] : rows[1], :]
        for _, _, which, rows in kinds
    ]
    items = make_reducers([kind[:2] for kind in kinds], grads, saved, refs[21:]) if kinds else []
    row_count, _, tokens, half = query.shape
    tile_count = held.shape[1]
    tiles, peers = plane_peers()
    low = jnp.bfloat16
    x, core = lax.axis_index("ty") // 2, lax.rem(lax.axis_index("ty"), 2)

    def group(which, base=0):
        return pl.ds(pl.multiple_of(base + which * half, 128), half)

    loads = []
    for row in range(row_count):
        loads.append([])
        for k, (source, target) in enumerate((
            (all_pairs.at[row], held.at[row]), (query_in.at[row], query.at[row]), (attended_in.at[row], attended.at[row]),
            (grad_in.at[x, row], grad.at[row, 0]), (lse_in.at[row], lse.at[row]),
        )):
            load = pltpu.make_async_copy(source, target, row_sem.at[row, k])
            load.start()
            loads[-1].append(load)
    greet([plane_peer(k)[0] for k in range(1, tile_count)] + (chip_peers()["z"] if kinds else []))
    chunk = 2
    flights = [{} for _ in range(row_count)]

    def send(row, slot, source, target, peer):
        copy = pltpu.make_async_remote_copy(
            src_ref=source,
            dst_ref=target,
            send_sem=send_sem.at[row, slot],
            recv_sem=recv_sem.at[row, slot],
            device_id=peer,
            device_id_type=MESH,
        )
        copy.start()
        flights[row][slot] = copy

    def compute(row):
        for load in loads[row]:
            load.wait()
        flights[row][8].wait()
        for t, name in enumerate(("own", "x")):
            fill_mask(mask.at[t], cuts, row, tiles[name], tile_height, tile_width)

        def one_pair(p, carry):
            at = pl.ds(pl.multiple_of(p * 128, 128), 128)
            at_value = pl.ds(pl.multiple_of(half + p * 128, 128), 128)
            boths, both_grads, deltas, levels = [], [], [], []
            for t in range(2):
                grad_pair = grad[row, t, :, at]
                boths.append(two_heads(query[row, t, :, at], 0.125))
                both_grads.append(two_heads(grad_pair, 1.0))
                inner = jnp.transpose(grad_pair.astype(jnp.float32) * attended[row, t, :, at].astype(jnp.float32))
                heads = [inner[: inner.shape[0] // 2], inner[inner.shape[0] // 2 :]]
                deltas.append(jnp.concatenate([jnp.sum(head, axis=0, keepdims=True) for head in heads], axis=1))
                levels.append(lse[row, p, t])
            all_both = jnp.concatenate(boths, axis=0)
            all_grads = jnp.concatenate(both_grads, axis=0)
            query_part = jnp.zeros((128, 4 * tokens), jnp.float32)
            for c in range(tile_count // chunk):
                span = slice(c * chunk * tokens, (c + 1) * chunk * tokens)
                some = slice(c * chunk, (c + 1) * chunk)
                keys = held[row, some, :, at].reshape(chunk * tokens, 128)
                values = held[row, some, :, at_value].reshape(chunk * tokens, 128)
                weight_parts, score_parts = [], []
                for t in range(2):
                    extra = mask[t, span, :]
                    raw = mm(keys, boths[t], 1, 1) + jnp.concatenate([extra, extra], axis=1)
                    weights = jnp.exp(raw - levels[t])
                    weight_parts.append(weights.astype(low))
                    score_parts.append((weights * (mm(values, both_grads[t], 1, 1) - deltas[t])).astype(low))
                score_grad = jnp.concatenate(score_parts, axis=1)
                value_part = mm(jnp.concatenate(weight_parts, axis=1), all_grads, 1, 0)
                key_part = mm(score_grad, all_both, 1, 0)
                query_part = query_part + mm(keys, score_grad, 0, 0)
                terms[row, some, :, at] = key_part.astype(low).reshape(chunk, tokens, 128)
                terms[row, some, :, at_value] = value_part.astype(low).reshape(chunk, tokens, 128)
            for t in range(2):
                blocks = own_blocks(query_part[:, 2 * t * tokens : 2 * (t + 1) * tokens]) * 0.125
                query_grad[row, t, :, at] = jnp.transpose(blocks).astype(low)
            return carry

        lax.fori_loop(0, half // 128, one_pair, 0)

    names = ("own", "x", "y", "xy")

    def begin(row):
        other = 2 - 4 * core
        for k in (3, 2, 1, 0):
            send(row, k, terms.at[row, tiles[names[k]] + other], core_terms.at[row, k], peers["core"])
        send(row, 7, query_grad.at[row, 1], x_query.at[row], peers["x"])

    def add(target, source):
        def body(i, carry):
            at = pl.ds(pl.multiple_of(i * 16, 16), 16)
            target[at, :] = target[at, :] + source[at, :]
            return carry

        lax.fori_loop(0, tokens // 16, body, 0)

    def scatter(row):
        for k in (3, 2, 1, 0):
            flights[row][k].wait()
            tile = terms.at[row, tiles[names[k]]]
            add(tile, core_terms.at[row, k])
            if k == 3:
                send(row, 5, tile, y_terms.at[row, 1], peers["y"])
            if k == 2:
                send(row, 4, tile, y_terms.at[row, 0], peers["y"])

    def pass_on(row):
        flights[row][5].wait()
        tile = terms.at[row, tiles["x"]]
        add(tile, y_terms.at[row, 1])
        send(row, 6, tile, x_terms.at[row], peers["x"])

    def close(row):
        for slot in (4, 6, 7):
            flights[row][slot].wait()
        mine = terms.at[row, tiles["own"]]
        width = 2 * half

        def body(i, carry):
            at = pl.ds(pl.multiple_of(i * 16, 16), 16)
            total = mine[at, :].astype(jnp.float32) + y_terms[row, 0, at, :].astype(jnp.float32)
            total = total.astype(low)
            out[row, at, group(x)] = query_grad[row, 0, at, :]
            out[row, at, group(x, width)] = total[:, :half]
            out[row, at, group(x, 2 * width)] = total[:, half:]
            out[row, at, group(1 - x)] = x_query[row, at, :]
            out[row, at, group(1 - x, width)] = x_terms[row, at, :half]
            out[row, at, group(1 - x, 2 * width)] = x_terms[row, at, half : 2 * half]
            return carry

        lax.fori_loop(0, tokens // 16, body, 0)

    part_copies = []

    def convolve():
        fill_shift(shift, tile_height, tile_width)
        patch = part.shape[2]
        taps[...] = mm(conv_turned[...], conv_in[...], 1, 1)
        rows = []
        for row in range(row_count):
            pieces = []
            for p in range(9):
                piece = taps[p * patch : (p + 1) * patch, row * tokens : (row + 1) * tokens]
                pieces.append(piece * same_image(cuts, row, p, tile_height, tile_width))
            rows.append(jnp.concatenate(pieces, axis=1))
        whole = jnp.concatenate(rows, axis=0)
        coarse = whole.astype(low)
        fine = (whole - coarse.astype(jnp.float32)).astype(low)
        moved = mm(coarse, shift[...], 1, 1) + mm(fine, shift[...], 1, 1)
        for tile in range(tile_count):
            part[tile] = moved[:, tile * tokens : (tile + 1) * tokens].reshape(row_count, patch, tokens)
        for k in range(1, tile_count):
            peer, tile = plane_peer(k)
            copy = pltpu.make_async_remote_copy(
                src_ref=part.at[tile],
                dst_ref=part_got.at[k],
                send_sem=part_send_sem.at[k],
                recv_sem=part_recv_sem.at[k],
                device_id=peer,
                device_id_type=MESH,
            )
            copy.start()
            part_copies.append(copy)
        conv_grad[...] = mm(conv_in[...], spread[...], 0, 1)

    def collect():
        total = part[tiles["own"]]
        for k, copy in enumerate(part_copies):
            copy.wait()
            total = total + part_got[k + 1]
        conv_out[...] = total.astype(low)

    def sum_up(item):
        item.step()
        item.save()

    for row in range(row_count):
        send(row, 8, grad_in.at[1 - x, row], grad.at[row, 1], peers["x"])
    for item in items:
        item.begin()
    acts = {"compute": compute, "begin": begin, "scatter": scatter, "pass": pass_on}
    if items and row_count == 3:
        order = list(back_order)
    else:
        rows = range(row_count)
        order = [f"{act}{row}" for row in rows for act in ("compute", "begin")]
        order += [f"scatter{row}" for row in rows] + [f"pass{row}" for row in rows] + ["convolve"]
    named = dict(zip(("fc1", "fc2a", "fc2b", "proj"), items))
    for entry in order:
        if entry == "convolve":
            convolve()
        elif entry[0] == "+":
            named[entry[1:]].step()
        elif entry[0] == "=":
            sum_up(named[entry[1:]])
        else:
            acts[entry[:-1]](int(entry[-1]))
    for row in range(row_count):
        close(row)
    collect()
    for item in items:
        item.land("save")


def attend_back(cuts, query, attended, grad, lse, conv_in, conv_turned, spread, all_pairs, grads, tile_height, tile_width):
    row_count, _, tokens, half = query.shape
    width = 2 * half
    kinds, sources, saves, shapes = [], [], [], []
    for start, paired, entry, rows in grads:
        if not any(entry is source for source in sources):
            sources.append(entry)
        which = [entry is source for source in sources].index(True)
        kinds.append((start, paired, which, rows))
        depth = entry.shape[1] if rows is None else rows[1] - rows[0]
        shapes.append((depth, entry.shape[2] if paired else entry.shape[2] // 2))
        saves.append((depth if start == "z" else depth // 4, shapes[-1][1]))
    kinds = tuple(kinds)
    tile_count = all_pairs.shape[1]
    taps = conv_turned.shape[0]
    low, wide = jnp.bfloat16, jnp.float32
    vmem, anywhere = pl.BlockSpec(memory_space=pltpu.VMEM), pl.BlockSpec(memory_space=pl.ANY)
    return pl.pallas_call(
        functools.partial(attend_back_kernel, tile_height, tile_width, kinds),
        out_shape=[
            jax.ShapeDtypeStruct((row_count, tokens, 3 * width), low),
            jax.ShapeDtypeStruct((width, taps), wide),
            jax.ShapeDtypeStruct((row_count, taps // 9, tokens), low),
        ]
        + [jax.ShapeDtypeStruct(s, low) for s in saves],
        in_specs=[pl.BlockSpec(memory_space=pltpu.SMEM)] + [anywhere] * 4 + [vmem] * 3 + [anywhere] * (1 + len(sources)),
        out_specs=[vmem] * 3 + [anywhere] * len(saves),
        scratch_shapes=[
            pltpu.VMEM(query.shape, low),
            pltpu.VMEM(query.shape, low),
            pltpu.VMEM(query.shape, low),
            pltpu.VMEM(lse.shape, wide),
            pltpu.SemaphoreType.DMA((row_count, 5)),
            pltpu.VMEM((row_count, tile_count, tokens, width), low),
            pltpu.VMEM((row_count, tile_count, tokens, width), low),
            pltpu.VMEM((row_count, 4, tokens, width), low),
            pltpu.VMEM((row_count, 2, tokens, width), low),
            pltpu.VMEM((row_count, tokens, width), low),
            pltpu.VMEM((row_count, tokens, half), low),
            pltpu.VMEM(query.shape, low),
            pltpu.VMEM((2, tile_count * tokens, tokens), wide),
            pltpu.VMEM((tile_count * tokens, 9 * tokens), low),
            pltpu.VMEM((taps, row_count * tokens), wide),
            pltpu.VMEM((tile_count, row_count, taps // 9, tokens), wide),
            pltpu.VMEM((tile_count, row_count, taps // 9, tokens), wide),
            pltpu.SemaphoreType.DMA((row_count, 9)),
            pltpu.SemaphoreType.DMA((row_count, 9)),
            pltpu.SemaphoreType.DMA((tile_count,)),
            pltpu.SemaphoreType.DMA((tile_count,)),
        ]
        + (reducer_scratch([kind[:2] for kind in kinds], shapes) if kinds else []),
        compiler_params=pltpu.CompilerParams(
            collective_id=2, has_side_effects=True, vmem_limit_bytes=full_vmem
        ),
        name="attend_back",
    )(cuts, query, attended, grad, lse, conv_in, conv_turned, spread, all_pairs, *sources)


def add_rows(target, first, second, rows):
    def body(i, carry):
        at = pl.ds(pl.multiple_of(i * 16, 16), 16)
        target[at, :] = first[at, :] + second[at, :]
        return carry

    lax.fori_loop(0, rows // 16, body, 0)


def add_four(target, others, rows):
    def body(i, carry):
        at = pl.ds(pl.multiple_of(i * 16, 16), 16)
        total = target[at, :].astype(jnp.float32) + others[0, at, :].astype(jnp.float32)
        total = total + (others[1, at, :].astype(jnp.float32) + others[2, at, :].astype(jnp.float32))
        target[at, :] = total.astype(jnp.bfloat16)
        return carry

    lax.fori_loop(0, rows // 16, body, 0)


def chip_peers():
    z, ty, y = lax.axis_index("rows"), lax.axis_index("ty"), lax.axis_index("tx")
    core, x = lax.rem(ty, 2), ty // 2
    across = (1 - x) * 2 + core
    return {
        "core": (z, x * 2 + 1 - core, y),
        "x": (z, across, y),
        "y": (z, ty, 1 - y),
        "xy": (z, across, 1 - y),
        "z": [(lax.rem(z + k, 4), ty, y) for k in (1, 2, 3)],
    }


class Reducer:
    def __init__(self, start, paired, relays, grad, out, buffers, sems, w):
        self.relays = relays
        self.start, self.paired, self.grad, self.out, self.w = start, paired, grad, out, w
        self.local_sem, self.send_sem, self.recv_sem = sems
        self.z, ty, self.y = lax.axis_index("rows"), lax.axis_index("ty"), lax.axis_index("tx")
        self.core, self.x = lax.rem(ty, 2), ty // 2
        self.peers = chip_peers()
        self.flying = {}
        self.own = buffers[0]
        if start in ("plane", "z"):
            self.half, self.quarter, self.final = buffers[1:4]
            self.got = None if paired else buffers[4]
            self.depth, self.width = grad.shape[1], grad.shape[2] if paired else grad.shape[2] // 2
        else:
            self.depth, self.width = out.shape[1], out.shape[2]
        if start == "block":
            self.half, self.quarter = buffers[1:]
        share = [self.relay, self.pass_strip] if relays else [self.pass_strip]
        late = [self.begin_late, self.add_half_late, self.add_quarter_late, *share, self.end]
        self.stages = {
            "plane": [self.add_core, self.add_half, self.add_quarter, self.sum_z, self.gather_piece, *share, self.end],
            "z": [self.add_core, self.sum_z_first] + late,
            "block": late,
            "piece": [self.gather_piece, *share, self.end],
        }[start]

    def step(self):
        self.stages.pop(0)()

    def part(self, at):
        if self.start == "block":
            return self.own.at[at]
        return self.own.at[self.z, at]

    def send(self, slot, source, target, peer):
        copy = pltpu.make_async_remote_copy(
            src_ref=source,
            dst_ref=target,
            send_sem=self.send_sem.at[self.w, slot],
            recv_sem=self.recv_sem.at[self.w, slot],
            device_id=peer,
            device_id_type=MESH,
        )
        copy.start()
        return copy

    def keep(self, slot, source, target):
        copy = pltpu.make_async_copy(source, target, self.local_sem.at[self.w, slot])
        copy.start()
        return copy

    def land(self, name):
        for copy in self.flying.pop(name):
            copy.wait()

    def columns(self, which):
        return pl.ds(pl.multiple_of(which * self.width, 128), self.width)

    def rows(self, start, size):
        return pl.ds(pl.multiple_of(start, 16), size)

    def place(self, block, flip_x=False, flip_y=False):
        x = 1 - self.x if flip_x else self.x
        y = 1 - self.y if flip_y else self.y
        later = block // 2
        major = x + later * (y - x)
        minor = y + later * (x - y)
        return self.rows(major * (self.depth // 2) + minor * (self.depth // 4), self.depth // 4)

    def pieces(self, flip_x=False, flip_y=False):
        if self.start in ("plane", "piece"):
            return [self.place(self.z, flip_x, flip_y)]
        x = 1 - self.x if flip_x else self.x
        y = 1 - self.y if flip_y else self.y
        half, less, least = self.depth // 2, self.depth // 4, self.depth // 8
        return [self.rows(x * less + y * least, least), self.rows(half + y * less + x * least, least)]

    def begin(self):
        if self.start in ("block", "piece"):
            self.flying["load"] = [self.keep(0, self.grad, self.own)]
            return
        if self.paired:
            self.flying["core"] = [self.keep(0, self.grad, self.own)]
            return
        swap = self.send(0, self.grad.at[:, :, self.columns(1 - self.core)], self.got, self.peers["core"])
        mine = self.keep(0, self.grad.at[:, :, self.columns(self.core)], self.own)
        self.flying["core"] = [swap, mine]

    def add_core(self):
        self.land("core")
        if not self.paired:
            for block in range(4):
                add_rows(self.own.at[block], self.own.at[block], self.got.at[block], self.depth)
        if self.start == "z":
            self.flying["z"] = [
                self.send(5 + k, self.own.at[peer[0]], self.final.at[k], peer) for k, peer in enumerate(self.peers["z"])
            ]
            return
        part = self.depth // 2
        first = self.send(1, self.own.at[0:2, self.rows((1 - self.x) * part, part)], self.half.at[0:2], self.peers["x"])
        second = self.send(2, self.own.at[2:4, self.rows((1 - self.y) * part, part)], self.half.at[2:4], self.peers["y"])
        self.flying["half"] = [first, second]

    def add_half(self):
        self.land("half")
        part, less = self.depth // 2, self.depth // 4
        for block in range(4):
            side = self.x if block < 2 else self.y
            kept = self.own.at[block, self.rows(side * part, part)]
            add_rows(kept, kept, self.half.at[block], part)
        first = self.own.at[0:2, self.rows(self.x * part + (1 - self.y) * less, less)]
        second = self.own.at[2:4, self.rows(self.y * part + (1 - self.x) * less, less)]
        self.flying["quarter"] = [
            self.send(3, first, self.quarter.at[0:2], self.peers["y"]),
            self.send(4, second, self.quarter.at[2:4], self.peers["x"]),
        ]

    def add_quarter(self):
        self.land("quarter")
        for block in range(4):
            kept = self.own.at[block, self.place(block // 2 * 2)]
            add_rows(kept, kept, self.quarter.at[block], self.depth // 4)
        self.flying["z"] = [
            self.send(5 + k, self.own.at[peer[0], self.place(peer[0])], self.final.at[k], peer)
            for k, peer in enumerate(self.peers["z"])
        ]

    def gather(self, pieces, sources):
        copies = []
        for n, (at, source) in enumerate(zip(pieces, sources)):
            target = self.out.at[self.core, at]
            for k, name in enumerate(("x", "y") if self.relays else ("x", "y", "xy")):
                copies.append(self.send(8 + 3 * n + k, source, target, self.peers[name]))
            copies.append(self.keep(1 + n, source, target))
        self.flying["gather"] = copies

    def relay(self):
        self.land("gather")
        cut = self.width // 256 * 128 + (128 if self.width % 256 and self.w % 2 else 0)
        copies = []
        for n, (from_x, from_y) in enumerate(zip(self.pieces(flip_x=True), self.pieces(flip_y=True))):
            first = self.out.at[self.core, from_x, pl.ds(0, cut)]
            second = self.out.at[self.core, from_y, pl.ds(cut, self.width - cut)]
            copies.append(self.send(14 + 2 * n + 1, first, first, self.peers["y"]))
            copies.append(self.send(14 + 2 * n + 2, second, second, self.peers["x"]))
        self.flying["relay"] = copies

    def sum_z(self):
        self.land("z")
        add_four(self.own.at[self.z, self.place(self.z)], self.final, self.depth // 4)

    def gather_piece(self):
        if self.start == "piece":
            self.land("load")
            self.gather([self.place(self.z)], [self.own])
        else:
            self.gather([self.place(self.z)], [self.own.at[self.z, self.place(self.z)]])

    def sum_z_first(self):
        self.land("z")
        add_four(self.own.at[self.z], self.final, self.depth)

    def save(self):
        source = self.own.at[self.z] if self.start == "z" else self.own.at[self.z, self.place(self.z)]
        self.flying["save"] = [self.keep(1, source, self.out)]

    def begin_late(self):
        if self.start == "block":
            self.land("load")
        half, less = self.depth // 2, self.depth // 4
        self.flying["half"] = [
            self.send(1, self.part(self.rows((1 - self.x) * less, less)), self.half.at[0], self.peers["x"]),
            self.send(2, self.part(self.rows(half + (1 - self.y) * less, less)), self.half.at[1], self.peers["y"]),
        ]

    def add_half_late(self):
        self.land("half")
        half, less, least = self.depth // 2, self.depth // 4, self.depth // 8
        for n, start in enumerate((self.x * less, half + self.y * less)):
            kept = self.part(self.rows(start, less))
            add_rows(kept, kept, self.half.at[n], less)
        first = self.part(self.rows(self.x * less + (1 - self.y) * least, least))
        second = self.part(self.rows(half + self.y * less + (1 - self.x) * least, least))
        self.flying["quarter"] = [
            self.send(3, first, self.quarter.at[0], self.peers["y"]),
            self.send(4, second, self.quarter.at[1], self.peers["x"]),
        ]

    def add_quarter_late(self):
        self.land("quarter")
        least = self.depth // 8
        pieces = self.pieces()
        for n, at in enumerate(pieces):
            add_rows(self.part(at), self.part(at), self.quarter.at[n], least)
        self.gather(pieces, [self.part(at) for at in pieces])

    def pass_strip(self):
        self.land("relay" if self.relays else "gather")
        strip = self.out.at[self.core]
        self.flying["strip"] = [self.send(14, strip, strip, self.peers["core"])]

    def end(self):
        self.land("strip")


def reducer_scratch(kinds, shapes):
    buffers = []
    for (start, paired), (depth, half) in zip(kinds, shapes):
        sizes = {
            "plane": [(4, depth, half), (4, depth // 2, half), (4, depth // 4, half), (3, depth // 4, half)],
            "z": [(4, depth, half), (2, depth // 4, half), (2, depth // 8, half), (3, depth, half)],
            "block": [(depth, half), (2, depth // 4, half), (2, depth // 8, half)],
            "piece": [(depth // 4, half)],
        }[start]
        if not paired:
            sizes.append((4, depth, half))
        buffers += [pltpu.VMEM(size, jnp.bfloat16) for size in sizes]
    count = len(kinds)
    return buffers + [
        pltpu.SemaphoreType.DMA((count, 3)),
        pltpu.SemaphoreType.DMA((count, 19)),
        pltpu.SemaphoreType.DMA((count, 19)),
    ]


def make_reducers(kinds, grads, outs, scratch, relays=()):
    items, at = [], 0
    for w, ((start, paired), grad, out) in enumerate(zip(kinds, grads, outs)):
        size = {"plane": 4, "z": 4, "block": 3, "piece": 1}[start] + (0 if paired else 1)
        items.append(Reducer(start, paired, w in relays, grad, out, scratch[at : at + size], scratch[-3:], w))
        at = at + size
    return items


def sum_by_table(local_grads):
    band_count, column_count = lax.axis_size("ty"), lax.axis_size("tx")
    group_count = lax.axis_size("rows")
    tile_count = band_count * column_count
    table = jnp.concatenate([entry.reshape(group_count, -1) for entry in local_grads], axis=1)
    column_total = table.shape[1]
    padded_columns = -(-column_total // tile_count) * tile_count
    piece_width = padded_columns // tile_count
    table = table.reshape(group_count, tile_count, piece_width)
    shares = lax.psum_scatter(
        table.reshape(group_count * tile_count, piece_width),
        ("rows", "ty", "tx"),
        scatter_dimension=0,
        tiled=True,
    )
    summed = (
        lax.all_gather(shares.astype(jnp.bfloat16), ("ty", "tx"), axis=0, tiled=True)
        .astype(shares.dtype)
        .reshape(-1)
    )
    totals = []
    start_at = 0
    for entry in local_grads:
        length = entry.size // group_count
        shard_shape = (entry.shape[0] // group_count,) + entry.shape[1:]
        totals.append(summed[start_at : start_at + length].reshape(shard_shape))
        start_at = start_at + length
    return tuple(totals)


def shards(
    latent,
    skip_input,
    segment_ids,
    embed_weight,
    embed_bias,
    skip_weight,
    skip_bias,
    norm1_gain,
    norm1_bias,
    qkv_weight,
    proj_weight,
    proj_bias,
    norm2_gain,
    norm2_bias,
    fc1_weight,
    fc1_bias,
    fc2_weight,
    fc2_bias,
    conv_weight,
    cotangent,
):
    row_count, tile_height, tile_width, width = skip_input.shape
    patch = latent.shape[3]
    tokens = tile_height * tile_width
    token_count = row_count * tokens
    low = jnp.bfloat16
    wide = jnp.float32
    conv_turned = conv_weight.T
    flat_latent = latent.reshape(token_count, patch)
    flat_skip = skip_input.reshape(token_count, width)
    biases = (embed_bias, skip_bias, norm1_gain, norm1_bias, proj_bias, norm2_gain, norm2_bias, fc2_bias)
    embedded, stream, normed, query, pairs, cot, vectors, hidden_bias, cuts = front(
        segment_ids, flat_latent, cotangent.reshape(token_count, patch), embed_weight.T, biases, fc1_bias,
        flat_skip, skip_weight, qkv_weight, row_count,
    )
    attended, log_total, held_query, held_attended, held_pairs, spread, out_grad, active_grad = attend(
        cuts, query, pairs, cot, conv_turned, fc2_weight, tile_height, tile_width
    )
    here = (lax.axis_size("rows"), lax.axis_size("ty"), lax.axis_size("tx")) == (4, 4, 2)
    fc1_grad, fc2_grad, hidden_bias_grad, proj_grad, attended_grad, mid_grad, conv_in, middle_grads = middle(
        attended.reshape(2, token_count, width // 2), stream, out_grad, active_grad, proj_weight, vectors, hidden_bias,
        fc1_weight, fc2_weight, here,
    )
    early = []
    if here:
        fc2_blocks = fc2_grad.reshape(4, -1, width // 2)
        middle_row = fc2_blocks.shape[1] // 2
        early = [
            ("plane", True, fc1_grad, None),
            ("z", True, fc2_blocks, (0, middle_row)),
            ("plane", True, fc2_blocks, (middle_row, 2 * middle_row)),
            ("plane", False, proj_grad.reshape(4, -1, width), None),
        ]
    projected_grad, conv_grad, conv_out, *saved = attend_back(
        cuts, held_query, held_attended, attended_grad.reshape(2, row_count, tokens, width // 2), log_total,
        conv_in, conv_turned, spread, held_pairs, early, tile_height, tile_width,
    )
    follow = {"plane": "piece", "z": "block"}
    resumed = [
        (follow[start], entry, (entry.shape[0] if start == "z" else 4 * entry.shape[0], entry.shape[1]))
        for (start, _, _, _), entry in zip(early, saved)
    ]
    skip_input_grad, *rest = rear(
        projected_grad.reshape(token_count, 3 * width), qkv_weight, normed, stream, mid_grad, embedded, flat_skip,
        skip_weight, flat_latent, vectors, middle_grads, hidden_bias_grad, conv_grad, resumed, here,
    )
    skip_input_grad = skip_input_grad.reshape(row_count, tile_height, tile_width, width)
    taps = 9 * patch
    share = width // 4
    if here:
        half = width // 2
        places = [(0, 0, half, 0), (1, 0, half, 0), (1, middle_row, half, 0), (2, 0, half, 0)]
        places += [(3, 0, half, k * width) for k in range(3)] + [(4, 0, half, 0)]
        totals = finish([place + (entry,) for place, entry in zip(places, rest[:8])], rest[8], rest[9], conv_out)
        fc1_total, fc2_total, proj_total, qkv_total, skip_total, embed_turned, conv_grad_turned = totals[:7]
        line, fc1_line = totals[7:15], totals[15]
        output = totals[16].reshape(row_count, tile_height, tile_width, patch)
        return (
            output, skip_input_grad, embed_turned.T, line[0], skip_total, line[1], line[2], line[3], qkv_total,
            proj_total, line[4], line[5], line[6], fc1_total, fc1_line, fc2_total, line[7], conv_grad_turned.T,
        )
    output = conv_out.transpose(0, 2, 1).reshape(row_count, tile_height, tile_width, patch)
    qkv_grad = jnp.concatenate([entry.reshape(-1, width) for entry in rest[:3]], axis=1)
    skip_grad, thin = [entry.reshape(-1, entry.shape[2]) for entry in rest[3:5]]
    flat = rest[5]
    fc1_grad = fc1_grad.reshape(width, -1)
    line = [flat[:, k, :share].reshape(-1) for k in range(8)]
    fc1_line = flat[:, 8:11].reshape(-1)
    local_grads = [
        thin[:, taps : taps + patch], line[0], skip_grad, line[1], line[2], line[3], qkv_grad, proj_grad, line[4],
        line[5], line[6], fc1_grad, fc1_line, fc2_grad, line[7], thin[:, :taps],
    ]
    return (output, skip_input_grad) + sum_by_table([entry.astype(wide) for entry in local_grads])


def solution(mesh):
    return jax.shard_map(
        shards,
        mesh=mesh,
        in_specs=(
            P("rows", "ty", "tx", None),
            P("rows", "ty", "tx", None),
            P("rows", None, None),
            P(),
            P(),
            P(),
            P(),
            P(),
            P(),
            P(),
            P(),
            P(),
            P(),
            P(),
            P(),
            P(),
            P(),
            P(),
            P(),
            P("rows", "ty", "tx", None),
        ),
        out_specs=(
            P("rows", "ty", "tx", None),
            P("rows", "ty", "tx", None),
            P("rows", None),
            P("rows"),
            P("rows", None),
            P("rows"),
            P("rows"),
            P("rows"),
            P("rows", None),
            P("rows", None),
            P("rows"),
            P("rows"),
            P("rows"),
            P("rows", None),
            P("rows"),
            P("rows", None),
            P("rows"),
            P("rows", None),
        ),
        check_vma=False,
    )
```

profile of v0, /device:TPU:0, one launch (start us, length us, event | category | flops | bytes accessed | tf_op | source)
XLA Modules:
  0.0 224.1 jit_solution(2790289717291746225)
XLA Ops:
  0.7 7.7 %front.1 = (bf16[384,768]{1,0:T(8,128)(2,1)}, f32[384,768]{1,0:T(8,128)}, bf16[384,768]{1,0:T(8,128)(2,1)}, bf16[2,3,128,384]{3,2,1,0:T(8,128)(2,1)}, bf16[2,3,1...) custom-call(s32[3,32,32]{2,1,0:T(8,128)} %segment_ids.1, ...), custom_call_target="tpu_custom_call" | custom-call | tf_op jit(solution)/shard_map/front/pallas_call | solution.py:136
  8.4 45.4 %attend.1 = (bf16[2,3,128,384]{3,2,1,0:T(8,128)(2,1)}, f32[3,3,2,1,256]{4,3,2,1,0:T(1,128)}, bf16[3,2,128,384]{3,2,1,0:T(8,128)(2,1)}, bf16[3,2,128,384]{3,2,1,0...) custom-call(s32[3,2]{1,0:T(4,128)} %get-tuple-element.78.cuts, ...), custom_call_target="tpu_custom_call" | custom-call | tf_op jit(solution)/shard_map/attend/pallas_call | solution.py:846
  53.8 27.7 %middle.1 = (bf16[4,192,1536]{2,1,0:T(8,128)(2,1)}, bf16[3072,384]{1,0:T(8,128)(2,1)}, f32[4,1,768]{2,1,0:T(1,128)}, bf16[768,768]{1,0:T(8,128)(2,1)}, bf16[2,38...) custom-call(bf16[2,384,384]{2,1,0:T(8,128)(2,1)} %bitcast.22, ...), custom_call_target="tpu_custom_call" | custom-call | tf_op jit(solution)/shard_map/middle/pallas_call | solution.py:350
  81.5 73.1 %attend_back.1 = (bf16[3,128,2304]{2,1,0:T(8,128)(2,1)}, f32[768,144]{1,0:T(8,128)}, bf16[3,16,128]{2,1,0:T(8,128)(2,1)}, bf16[48,1536]{1,0:T(8,128)(2,1)}, bf16...) custom-call(s32[3,2]{1,0:T(4,128)} %get-tuple-element.78.cuts, ...), custom_call_target="tpu_custom_call" | custom-call | tf_op jit(solution)/shard_map/attend_back/pallas_call | solution.py:1132
  154.6 62.0 %rear.1 = (bf16[384,768]{1,0:T(8,128)(2,1)}, bf16[2,192,1536]{2,1,0:T(8,128)(2,1)}, bf16[2,384,384]{2,1,0:T(8,128)(2,1)}, bf16[2,384,384]{2,1,0:T(8,128)(2,1)}, ...) custom-call(bf16[384,2304]{1,0:T(8,128)(2,1)} %bitcast.17, ...), custom_call_target="tpu_custom_call" | custom-call | tf_op jit(solution)/shard_map/rear/pallas_call | solution.py:510
  216.6 0.0 copy-start
  216.7 6.6 %finish.1 = (f32[192,3072]{1,0:T(8,128)}, f32[768,768]{1,0:T(8,128)}, f32[192,768]{1,0:T(8,128)}, f32[192,2304]{1,0:T(8,128)}, f32[384,768]{1,0:T(8,128)}, /*ind...) custom-call(bf16[2,192,1536]{2,1,0:T(8,128)(2,1)} %get-tuple-element, ...), custom_call_target="tpu_custom_call" | custom-call | tf_op jit(solution)/shard_map/finish/pallas_call | solution.py:576
  223.3 0.0 copy-done
  223.3 0.8 copy.39
Async XLA Ops:
  216.6 6.6 %copy-start = (bf16[384,768]{1,0:T(8,128)(2,1)S(1)}, bf16[384,768]{1,0:T(8,128)(2,1)}, u32[]{:S(2)}) copy-start(bf16[384,768]{1,0:T(8,128)(2,1)} %get-tuple-element.121) | copy-start | bytes 1769476
where the time goes:
time: 224 us
  Pallas kernels  223 us (100%)
    pallas_call x1, Pallas kernels, attend_back(): pl.pallas_call(functools.partial(attend_back_kernel, tile_height, tile_wi...  73.1 us
    pallas_call x1, Pallas kernels, rear(): pl.pallas_call(functools.partial(rear_kernel, kinds, reduces), out_shape=...  62 us
    pallas_call x1, Pallas kernels, attend(): pl.pallas_call(functools.partial(attend_kernel, tile_height, tile_width),...  45.4 us
    pallas_call x1, Pallas kernels, middle(): pl.pallas_call(functools.partial(middle_kernel, paired), grid=(steps,), o...  27.7 us
    pallas_call x1, Pallas kernels, front(): pl.pallas_call(front_kernel, out_shape=[jax.ShapeDtypeStruct((token_count...  7.74 us
    pallas_call x1, Pallas kernels, finish(): pl.pallas_call(functools.partial(finish_kernel, patch, plan), out_shape=[...  6.61 us

commit v1 on v0

--- a/solution.py
+++ b/solution.py
@@ -180,24 +180,26 @@
     parts = [slice(0, token_count)]
     store_sem = refs[-1]
     if paired:
-        got1, got2, total1, total2, send_sem, recv_sem = refs[:6]
+        got1, got2, total1, total2, half_got, send_sem, recv_sem, half_send, half_recv = refs[:9]
         z, ty, y = lax.axis_index("rows"), lax.axis_index("ty"), lax.axis_index("tx")
         core = lax.rem(ty, 2)
         peer = (z, ty + 1 - 2 * core, y)
+        x = ty // 2
+        sides = (x, x, y, y)
+        peer_x, peer_y = (z, (1 - x) * 2 + core, y), (z, ty, 1 - y)
+
+    def store(k, which):
+        slot = lax.rem(k, 2)
+        if which == 0:
+            source = total1 if paired else grad1
+            target = fc1_out.at[:, :, pl.ds(pl.multiple_of(k * source.shape[3], 128), source.shape[3])]
+        else:
+            source = total2 if paired else grad2
+            target = fc2_out.at[pl.ds(pl.multiple_of(k * source.shape[1], 16), source.shape[1])]
+        return pltpu.make_async_copy(source.at[slot], target, store_sem.at[slot, which])
 
     def stores(k):
-        slot = lax.rem(k, 2)
-        first, second = (total1, total2) if paired else (grad1, grad2)
-        across = first.shape[3]
-        down = second.shape[1]
-        return [
-            pltpu.make_async_copy(
-                first.at[slot], fc1_out.at[:, :, pl.ds(pl.multiple_of(k * across, 128), across)], store_sem.at[slot, 0]
-            ),
-            pltpu.make_async_copy(
-                second.at[slot], fc2_out.at[pl.ds(pl.multiple_of(k * down, 16), down)], store_sem.at[slot, 1]
-            ),
-        ]
+        return [store(k, 0), store(k, 1)]
 
     def swaps(k):
         slot = lax.rem(k, 2)
@@ -216,6 +218,34 @@
             for n, (source, target) in enumerate(pairs)
         ]
 
+    def halves(k):
+        slot = lax.rem(k, 2)
+        part = total1.shape[2] // 2
+        copies = []
+        for n, (side, other) in enumerate(((x, peer_x), (y, peer_y))):
+            theirs = pl.ds(pl.multiple_of((1 - side) * part, 16), part)
+            copies.append(
+                pltpu.make_async_remote_copy(
+                    src_ref=total1.at[slot, 2 * n : 2 * n + 2, theirs],
+                    dst_ref=half_got.at[k, 2 * n : 2 * n + 2],
+                    send_sem=half_send.at[k, n],
+                    recv_sem=half_recv.at[k, n],
+                    device_id=other,
+                    device_id_type=MESH,
+                )
+            )
+        return copies
+
+    def late(k):
+        slot = lax.rem(k, 2)
+        part = total1.shape[2] // 2
+        for copy in halves(k):
+            copy.wait()
+        for n in range(4):
+            kept = pl.ds(pl.multiple_of(sides[n] * part, 16), part)
+            total1[slot, n, kept, :] = total1[slot, n, kept, :] + half_got[k, n]
+        store(k, 0).start()
+
     def settle(k):
         slot = lax.rem(k, 2)
         if paired:
@@ -231,13 +261,24 @@
             mine2 = pl.ds(pl.multiple_of(core * (width // 2), 128), width // 2)
             total1[slot] = grad1[slot, :, :, mine1] + got1[k]
             total2[slot] = grad2[slot, :, mine2] + got2[k]
-        for copy in stores(k):
-            copy.start()
+            store(k, 1).start()
+
+            @pl.when(k < last)
+            def _():
+                for copy in halves(k):
+                    copy.start()
+
+            @pl.when(k == last)
+            def _():
+                store(k, 0).start()
+        else:
+            for copy in stores(k):
+                copy.start()
 
     @pl.when(step == 0)
     def _():
         if paired:
-            greet([peer])
+            greet([peer, peer_x, peer_y])
         total = jnp.zeros((1, width), jnp.float32)
         for at in parts:
             grad = out_grad[at, :]
@@ -281,6 +322,10 @@
     if paired:
         for copy in swaps(step):
             copy.start()
+
+        @pl.when(step > 1)
+        def _():
+            late(step - 2)
 
         @pl.when(step > 0)
         def _():
@@ -313,6 +358,7 @@
         vector_grads[5:6] = gain_sum
         vector_grads[6:7] = bias_sum
         if paired:
+            late(last - 1)
             settle(step)
         for k in (last - 1, last):
             for copy in stores(k):
@@ -341,6 +387,9 @@
             pltpu.VMEM((steps, block, width // 2), low),
             pltpu.VMEM((2, 4, width // 4, block // 2), low),
             pltpu.VMEM((2, block, width // 2), low),
+            pltpu.VMEM((steps, 4, width // 8, block // 2), low),
+            pltpu.SemaphoreType.DMA((steps, 2)),
+            pltpu.SemaphoreType.DMA((steps, 2)),
             pltpu.SemaphoreType.DMA((steps, 2)),
             pltpu.SemaphoreType.DMA((steps, 2)),
         ]
@@ -374,16 +423,6 @@
     )(attended, stream, out_grad, proj_weight, vectors, hidden_bias, active_grad, fc1_weight, fc2_weight)
 
 
-rear_order = (
-    "+proj", "+fc2b", "+fc2a", "grad0", "grad1", "grad2", "+qkv0", "+qkv2", "norm", "+qkv0", "+qkv1", "skip",
-    "+qkv0", "+qkv2", "+skip", "joined", "+qkv2", "+thin", "+proj", "+qkv1", "+skip", "+thin", "+qkv1", "+fc1",
-    "=qkv0", "+fc2b", "+proj", "+skip", "+flat", "+thin", "+fc2a", "=qkv1", "=qkv2", "+qkv0", "+fc1", "+qkv1",
-    "+fc2a", "+flat", "+fc2b", "+qkv2", "=skip", "+qkv1", "+fc2a", "+proj", "+fc2b", "+flat", "+qkv0", "+fc1",
-    "input", "+qkv0", "=thin", "=flat", "+fc1", "+qkv1", "+qkv2", "+skip", "+fc2a", "+thin", "+flat", "+qkv2",
-    "+fc2a", "+flat", "+skip", "+thin",
-)
-
-
 def rear_kernel(
     kinds, reduces, projected_in, qkv_in, normed_in, stream_in, mid_in, embedded_in, skip_in, skip_weight_in,
     latent, vectors, middle_grads, hidden_bias_grad, conv_grad, *refs
@@ -402,23 +441,23 @@
     loads = [pltpu.make_async_copy(a, b, load_sem.at[k]) for k, (a, b) in enumerate(zip(sources, targets))]
     for load in loads[:3]:
         load.start()
-    named = {}
+    items = [None] * 10
     if reduces:
         items = make_reducers(kinds + (("plane", False),) * 6, resumed + grads, sums, refs[10:], range(count + 3))
-        named = dict(zip(("fc1", "fc2a", "fc2b", "proj", "qkv0", "qkv1", "qkv2", "skip", "thin", "flat"), items))
         greet([peers[name] for name in ("core", "x", "y", "xy")] + peers["z"])
         for item in items[:count]:
             item.begin()
+    fc1, fc2a, fc2b, proj, qkv0, qkv1, qkv2, skips, thins, flats = items
     for load in loads[3:]:
         load.start()
     width = stream.shape[1]
     low = jnp.bfloat16
     made = {}
 
-    def open_up(*names):
-        for name in names:
+    def open_up(*some):
+        for item in some:
             if reduces:
-                named[name].begin()
+                item.begin()
 
     def weight_grad(k):
         if k == 0:
@@ -426,7 +465,7 @@
             loads[1].wait()
         piece = mm(normed[...], projected_grad[:, k * width : (k + 1) * width], 0, 0)
         grads[k][...] = piece.astype(low).reshape(grads[k].shape)
-        open_up(f"qkv{k}")
+        open_up((qkv0, qkv1, qkv2)[k])
 
     def norm():
         for load in loads[2:5]:
@@ -442,7 +481,7 @@
         loads[6].wait()
         skip_grad[0:2] = mm(embedded[...], stream_low[...], 0, 0).astype(low).reshape(2, width // 2, width)
         skip_grad[2:4] = mm(skip[...], stream_low[...], 0, 0).astype(low).reshape(2, width // 2, width)
-        open_up("skip")
+        open_up(skips)
 
     def joined():
         loads[7].wait()
@@ -464,23 +503,36 @@
             body = jnp.concatenate([own] + pieces + [jnp.zeros((8 - len(pieces), 256), jnp.float32)], axis=0)
             flat[block, 0:16] = body.astype(low)
             flat[block, 16:64] = jnp.zeros((48, 256), low)
-        open_up("thin", "flat")
+        open_up(thins, flats)
 
     def input_grad():
         skip_input_grad[...] = mm(stream_low[...], skip_weight[width:], 1, 1).astype(low)
 
-    acts = {"norm": norm, "skip": skip_weight_grad, "joined": joined, "input": input_grad}
-    for entry in rear_order:
-        if entry[0] in "+=":
+    def advance(*some):
+        for item in some:
             if reduces:
-                named[entry[1:]].step()
-                if entry[0] == "=":
-                    named[entry[1:]].step()
-        elif entry[:-1] == "grad":
-            weight_grad(int(entry[-1]))
-        else:
-            acts[entry]()
-    assert not any(item.stages for item in named.values())
+                item.step()
+
+    advance(proj, fc2b, fc2a)
+    weight_grad(0)
+    weight_grad(1)
+    weight_grad(2)
+    advance(qkv0, qkv2)
+    norm()
+    advance(qkv0, qkv1)
+    skip_weight_grad()
+    advance(qkv0, qkv2, skips)
+    joined()
+    advance(qkv2, thins, proj, qkv1, skips, thins, qkv1, fc1)
+    advance(qkv0, qkv0, fc2b, proj, skips, flats, thins, fc2a)
+    advance(qkv1, qkv1, qkv2, qkv2, qkv0, fc1, qkv1, fc2a)
+    advance(flats, fc2b, qkv2, skips, skips, qkv1, fc2a, proj)
+    advance(fc2b, flats, qkv0, fc1)
+    input_grad()
+    advance(qkv0, thins, thins, flats, flats, fc1, qkv1, qkv2)
+    advance(skips, fc2a, thins, flats, qkv2, fc2a, flats, skips)
+    advance(thins)
+    assert not reduces or not any(item.stages for item in items)
 
 
 def rear(projected_grad, qkv_weight, normed, stream, mid_grad, embedded, skip, skip_weight, latent, vectors, middle_grads, hidden_bias_grad, conv_grad, resumed, reduces):
@@ -883,15 +935,8 @@
     )(cuts, query, pairs, cot, conv_turned, fc2_weight)
 
 
-back_order = (
-    "+fc2b", "+fc1", "compute0", "+fc2a", "begin0", "scatter0", "compute1", "+fc1", "begin1", "+proj", "compute2",
-    "+fc2b", "pass0", "+fc1", "+proj", "=fc2a", "begin2", "scatter1", "+fc2b", "scatter2", "convolve", "pass1",
-    "+proj", "pass2", "=fc2b", "=fc1", "=proj",
-)
-
-
 def attend_back_kernel(
-    tile_height, tile_width, kinds, cuts, query_in, attended_in, grad_in, lse_in, conv_in, conv_turned, spread,
+    tile_height, tile_width, kinds, done, cuts, query_in, attended_in, grad_in, lse_in, conv_in, conv_turned, spread,
     all_pairs, *refs
 ):
     count = max([kind[2] for kind in kinds], default=-1) + 1
@@ -906,6 +951,8 @@
         for _, _, which, rows in kinds
     ]
     items = make_reducers([kind[:2] for kind in kinds], grads, saved, refs[21:]) if kinds else []
+    for item, columns in zip(items, done):
+        item.halved = columns
     row_count, _, tokens, half = query.shape
     tile_count = held.shape[1]
     tiles, peers = plane_peers()
@@ -1088,26 +1135,50 @@
         send(row, 8, grad_in.at[1 - x, row], grad.at[row, 1], peers["x"])
     for item in items:
         item.begin()
-    acts = {"compute": compute, "begin": begin, "scatter": scatter, "pass": pass_on}
     if items and row_count == 3:
-        order = list(back_order)
+        fc1, fc2a, fc2b, proj = items
+        fc1.step()
+        fc2a.step()
+        proj.step()
+        fc2b.step()
+        compute(0)
+        fc1.step()
+        begin(0)
+        scatter(0)
+        compute(1)
+        begin(1)
+        fc2b.step()
+        proj.step()
+        scatter(1)
+        fc1.step()
+        compute(2)
+        pass_on(0)
+        proj.step()
+        begin(2)
+        scatter(2)
+        fc2b.step()
+        pass_on(1)
+        convolve()
+        sum_up(proj)
+        pass_on(2)
+        sum_up(fc1)
+        sum_up(fc2a)
+        sum_up(fc2b)
+        for row in range(row_count):
+            close(row)
+        collect()
     else:
-        rows = range(row_count)
-        order = [f"{act}{row}" for row in rows for act in ("compute", "begin")]
-        order += [f"scatter{row}" for row in rows] + [f"pass{row}" for row in rows] + ["convolve"]
-    named = dict(zip(("fc1", "fc2a", "fc2b", "proj"), items))
-    for entry in order:
-        if entry == "convolve":
-            convolve()
-        elif entry[0] == "+":
-            named[entry[1:]].step()
-        elif entry[0] == "=":
-            sum_up(named[entry[1:]])
-        else:
-            acts[entry[:-1]](int(entry[-1]))
-    for row in range(row_count):
-        close(row)
-    collect()
+        for row in range(row_count):
+            compute(row)
+            begin(row)
+        for row in range(row_count):
+            scatter(row)
+        for row in range(row_count):
+            pass_on(row)
+        convolve()
+        for row in range(row_count):
+            close(row)
+        collect()
     for item in items:
         item.land("save")
 
@@ -1116,7 +1187,7 @@
     row_count, _, tokens, half = query.shape
     width = 2 * half
     kinds, sources, saves, shapes = [], [], [], []
-    for start, paired, entry, rows in grads:
+    for start, paired, entry, rows, _ in grads:
         if not any(entry is source for source in sources):
             sources.append(entry)
         which = [entry is source for source in sources].index(True)
@@ -1125,12 +1196,13 @@
         shapes.append((depth, entry.shape[2] if paired else entry.shape[2] // 2))
         saves.append((depth if start == "z" else depth // 4, shapes[-1][1]))
     kinds = tuple(kinds)
+    done = tuple(entry[4] for entry in grads)
     tile_count = all_pairs.shape[1]
     taps = conv_turned.shape[0]
     low, wide = jnp.bfloat16, jnp.float32
     vmem, anywhere = pl.BlockSpec(memory_space=pltpu.VMEM), pl.BlockSpec(memory_space=pl.ANY)
     return pl.pallas_call(
-        functools.partial(attend_back_kernel, tile_height, tile_width, kinds),
+        functools.partial(attend_back_kernel, tile_height, tile_width, kinds, done),
         out_shape=[
             jax.ShapeDtypeStruct((row_count, tokens, 3 * width), low),
             jax.ShapeDtypeStruct((width, taps), wide),
@@ -1205,7 +1277,7 @@
 
 class Reducer:
     def __init__(self, start, paired, relays, grad, out, buffers, sems, w):
-        self.relays = relays
+        self.relays, self.halved = relays, 0
         self.start, self.paired, self.grad, self.out, self.w = start, paired, grad, out, w
         self.local_sem, self.send_sem, self.recv_sem = sems
         self.z, ty, self.y = lax.axis_index("rows"), lax.axis_index("ty"), lax.axis_index("tx")
@@ -1303,8 +1375,10 @@
             ]
             return
         part = self.depth // 2
-        first = self.send(1, self.own.at[0:2, self.rows((1 - self.x) * part, part)], self.half.at[0:2], self.peers["x"])
-        second = self.send(2, self.own.at[2:4, self.rows((1 - self.y) * part, part)], self.half.at[2:4], self.peers["y"])
+        rest = pl.ds(self.halved, self.width - self.halved)
+        theirs = [self.rows((1 - side) * part, part) for side in (self.x, self.y)]
+        first = self.send(1, self.own.at[0:2, theirs[0], rest], self.half.at[0:2, :, rest], self.peers["x"])
+        second = self.send(2, self.own.at[2:4, theirs[1], rest], self.half.at[2:4, :, rest], self.peers["y"])
         self.flying["half"] = [first, second]
 
     def add_half(self):
@@ -1312,8 +1386,9 @@
         part, less = self.depth // 2, self.depth // 4
         for block in range(4):
             side = self.x if block < 2 else self.y
-            kept = self.own.at[block, self.rows(side * part, part)]
-            add_rows(kept, kept, self.half.at[block], part)
+            rest = pl.ds(self.halved, self.width - self.halved)
+            kept = self.own.at[block, self.rows(side * part, part), rest]
+            add_rows(kept, kept, self.half.at[block, :, rest], part)
         first = self.own.at[0:2, self.rows(self.x * part + (1 - self.y) * less, less)]
         second = self.own.at[2:4, self.rows(self.y * part + (1 - self.x) * less, less)]
         self.flying["quarter"] = [
@@ -1517,10 +1592,10 @@
         fc2_blocks = fc2_grad.reshape(4, -1, width // 2)
         middle_row = fc2_blocks.shape[1] // 2
         early = [
-            ("plane", True, fc1_grad, None),
-            ("z", True, fc2_blocks, (0, middle_row)),
-            ("plane", True, fc2_blocks, (middle_row, 2 * middle_row)),
-            ("plane", False, proj_grad.reshape(4, -1, width), None),
+            ("plane", True, fc1_grad, None, fc1_grad.shape[2] * 3 // 4),
+            ("z", True, fc2_blocks, (0, middle_row), 0),
+            ("plane", True, fc2_blocks, (middle_row, 2 * middle_row), 0),
+            ("plane", False, proj_grad.reshape(4, -1, width), None, 0),
         ]
     projected_grad, conv_grad, conv_out, *saved = attend_back(
         cuts, held_query, held_attended, attended_grad.reshape(2, row_count, tokens, width // 2), log_total,
@@ -1529,7 +1604,7 @@
     follow = {"plane": "piece", "z": "block"}
     resumed = [
         (follow[start], entry, (entry.shape[0] if start == "z" else 4 * entry.shape[0], entry.shape[1]))
-        for (start, _, _, _), entry in zip(early, saved)
+        for (start, *_), entry in zip(early, saved)
     ]
     skip_input_grad, *rest = rear(
         projected_grad.reshape(token_count, 3 * width), qkv_weight, normed, stream, mid_grad, embedded, flat_skip,

time: 224 us -> 217 us (0.969)
  Pallas kernels: 223 us -> 216 us
    pallas_call x1, Pallas kernels: 73.1 us -> 63.3 us  [attend_back(): pl.pallas_call(functools.partial(attend_back_kernel, tile_height, tile_wi...]
    pallas_call x1, Pallas kernels: 27.7 us -> 31.3 us  [middle(): pl.pallas_call(functools.partial(middle_kernel, paired), grid=(steps,), o...]
where the time goes in v1:
time: 217 us
  Pallas kernels  216 us (100%)
    pallas_call x1, Pallas kernels, attend_back(): pl.pallas_call(functools.partial(attend_back_kernel, tile_height, tile_wi...  63.3 us
    pallas_call x1, Pallas kernels, rear(): pl.pallas_call(functools.partial(rear_kernel, kinds, reduces), out_shape=...  61.2 us
    pallas_call x1, Pallas kernels, attend(): pl.pallas_call(functools.partial(attend_kernel, tile_height, tile_width),...  45.4 us
    pallas_call x1, Pallas kernels, middle(): pl.pallas_call(functools.partial(middle_kernel, paired), grid=(steps,), o...  31.3 us
    pallas_call x1, Pallas kernels, front(): pl.pallas_call(front_kernel, out_shape=[jax.ShapeDtypeStruct((token_count...  7.74 us
    pallas_call x1, Pallas kernels, finish(): pl.pallas_call(functools.partial(finish_kernel, patch, plan), out_shape=[...  6.61 us

profile of v1, /device:TPU:0, one launch (start us, length us, event | category | flops | bytes accessed | tf_op | source)
XLA Modules:
  0.0 217.1 jit_solution(12385074221918557394)
XLA Ops:
  0.7 7.7 %front.1 = (bf16[384,768]{1,0:T(8,128)(2,1)}, f32[384,768]{1,0:T(8,128)}, bf16[384,768]{1,0:T(8,128)(2,1)}, bf16[2,3,128,384]{3,2,1,0:T(8,128)(2,1)}, bf16[2,3,1...) custom-call(s32[3,32,32]{2,1,0:T(8,128)} %segment_ids.1, ...), custom_call_target="tpu_custom_call" | custom-call | tf_op jit(solution)/shard_map/front/pallas_call | solution.py:136
  8.4 45.4 %attend.1 = (bf16[2,3,128,384]{3,2,1,0:T(8,128)(2,1)}, f32[3,3,2,1,256]{4,3,2,1,0:T(1,128)}, bf16[3,2,128,384]{3,2,1,0:T(8,128)(2,1)}, bf16[3,2,128,384]{3,2,1,0...) custom-call(s32[3,2]{1,0:T(4,128)} %get-tuple-element.78.cuts, ...), custom_call_target="tpu_custom_call" | custom-call | tf_op jit(solution)/shard_map/attend/pallas_call | solution.py:898
  53.8 31.3 %middle.1 = (bf16[4,192,1536]{2,1,0:T(8,128)(2,1)}, bf16[3072,384]{1,0:T(8,128)(2,1)}, f32[4,1,768]{2,1,0:T(1,128)}, bf16[768,768]{1,0:T(8,128)(2,1)}, bf16[2,38...) custom-call(bf16[2,384,384]{2,1,0:T(8,128)(2,1)} %bitcast.22, ...), custom_call_target="tpu_custom_call" | custom-call | tf_op jit(solution)/shard_map/middle/pallas_call | solution.py:399
  85.1 63.3 %attend_back.1 = (bf16[3,128,2304]{2,1,0:T(8,128)(2,1)}, f32[768,144]{1,0:T(8,128)}, bf16[3,16,128]{2,1,0:T(8,128)(2,1)}, bf16[48,1536]{1,0:T(8,128)(2,1)}, bf16...) custom-call(s32[3,2]{1,0:T(4,128)} %get-tuple-element.78.cuts, ...), custom_call_target="tpu_custom_call" | custom-call | tf_op jit(solution)/shard_map/attend_back/pallas_call | solution.py:1204
  148.4 61.2 %rear.1 = (bf16[384,768]{1,0:T(8,128)(2,1)}, bf16[2,192,1536]{2,1,0:T(8,128)(2,1)}, bf16[2,384,384]{2,1,0:T(8,128)(2,1)}, bf16[2,384,384]{2,1,0:T(8,128)(2,1)}, ...) custom-call(bf16[384,2304]{1,0:T(8,128)(2,1)} %bitcast.17, ...), custom_call_target="tpu_custom_call" | custom-call | tf_op jit(solution)/shard_map/rear/pallas_call | solution.py:562
  209.6 0.0 copy-start
  209.6 6.6 %finish.1 = (f32[192,3072]{1,0:T(8,128)}, f32[768,768]{1,0:T(8,128)}, f32[192,768]{1,0:T(8,128)}, f32[192,2304]{1,0:T(8,128)}, f32[384,768]{1,0:T(8,128)}, /*ind...) custom-call(bf16[2,192,1536]{2,1,0:T(8,128)(2,1)} %get-tuple-element, ...), custom_call_target="tpu_custom_call" | custom-call | tf_op jit(solution)/shard_map/finish/pallas_call | solution.py:628
  216.3 0.0 copy-done
  216.3 0.8 copy.39
Async XLA Ops:
  209.6 6.6 %copy-start = (bf16[384,768]{1,0:T(8,128)(2,1)S(1)}, bf16[384,768]{1,0:T(8,128)(2,1)}, u32[]{:S(2)}) copy-start(bf16[384,768]{1,0:T(8,128)(2,1)} %get-tuple-element.121) | copy-start | bytes 1769476

commit v2 on v1

--- a/solution.py
+++ b/solution.py
@@ -278,7 +278,8 @@
     @pl.when(step == 0)
     def _():
         if paired:
-            greet([peer, peer_x, peer_y])
+            for other in (peer, peer_x, peer_y):
+                pl.semaphore_signal(pltpu.get_barrier_semaphore(), inc=1, device_id=other, device_id_type=MESH)
         total = jnp.zeros((1, width), jnp.float32)
         for at in parts:
             grad = out_grad[at, :]
@@ -320,6 +321,11 @@
     grad2[slot] = mm(jnp.concatenate(actives, axis=0), out_low[...], 0, 0).astype(low)
     grad1[slot] = mm(normed[...], jnp.concatenate(hidden_lows, axis=0), 0, 0).astype(low).reshape(grad1.shape[1:])
     if paired:
+
+        @pl.when(step == 0)
+        def _():
+            pl.semaphore_wait(pltpu.get_barrier_semaphore(), 3)
+
         for copy in swaps(step):
             copy.start()
 
@@ -572,16 +578,22 @@
 
 def finish_kernel(patch, plan, *refs):
     count = len(plan)
-    sums, (thin, flat, conv_out) = refs[:count], refs[count : count + 3]
-    totals, refs = refs[count + 3 : count + 8], refs[count + 8 :]
-    (embed_turned, conv_turned), lines, fc1_line, output, refs = refs[:2], refs[2:10], refs[10], refs[11], refs[12:]
-    lows, wides, load_sem, store_sem = refs[:count], refs[count : count + 5], refs[count + 5], refs[count + 6]
+    sums, (thin, flat, conv_out, passed) = refs[:count], refs[count : count + 4]
+    totals, refs = refs[count + 4 : count + 9], refs[count + 9 :]
+    (embed_turned, conv_turned), lines, fc1_line, output, handed, refs = refs[:2], refs[2:10], refs[10], refs[11], refs[12], refs[13:]
+    lows, wides, held, load_sem, store_sem = refs[:count], refs[count : count + 5], *refs[count + 5 :]
+    take = pltpu.make_async_copy(passed, held, load_sem.at[count])
+    give = pltpu.make_async_copy(held, handed, store_sem.at[count])
     loads = [pltpu.make_async_copy(a, b, load_sem.at[k]) for k, (a, b) in enumerate(zip(sums, lows))]
     for load in loads:
         load.start()
-    stores = []
+    take.start()
+    stores = [give]
     for k, (low, (which, start, piece, left)) in enumerate(zip(lows, plan)):
         loads[k].wait()
+        if k == 1:
+            take.wait()
+            give.start()
         wide = wides[which]
         half, depth = low.shape[2], low.shape[1]
 
@@ -614,7 +626,7 @@
         store.wait()
 
 
-def finish(sums, thin, flat, conv_out):
+def finish(sums, thin, flat, conv_out, passed):
     row_count, patch, tokens = conv_out.shape
     share = thin.shape[1]
     wide = jnp.float32
@@ -630,15 +642,17 @@
         out_shape=[jax.ShapeDtypeStruct(shape, wide) for shape in whole]
         + [jax.ShapeDtypeStruct((patch, share), wide), jax.ShapeDtypeStruct((9 * patch, share), wide)]
         + [jax.ShapeDtypeStruct((share,), wide)] * 8
-        + [jax.ShapeDtypeStruct((4 * share,), wide), jax.ShapeDtypeStruct((row_count, tokens, patch), jnp.bfloat16)],
-        in_specs=[anywhere] * len(arrays) + [vmem] * 3,
-        out_specs=[anywhere] * 5 + [vmem] * 12,
+        + [jax.ShapeDtypeStruct((4 * share,), wide), jax.ShapeDtypeStruct((row_count, tokens, patch), jnp.bfloat16)]
+        + [jax.ShapeDtypeStruct(passed.shape, passed.dtype)],
+        in_specs=[anywhere] * len(arrays) + [vmem] * 3 + [anywhere],
+        out_specs=[anywhere] * 5 + [vmem] * 12 + [anywhere],
         scratch_shapes=[pltpu.VMEM(entry.shape, jnp.bfloat16) for entry in arrays]
         + [pltpu.VMEM(shape, wide) for shape in whole]
-        + [pltpu.SemaphoreType.DMA((len(arrays),)), pltpu.SemaphoreType.DMA((len(arrays),))],
+        + [pltpu.VMEM(passed.shape, passed.dtype)]
+        + [pltpu.SemaphoreType.DMA((len(arrays) + 1,))] * 2,
         compiler_params=pltpu.CompilerParams(vmem_limit_bytes=full_vmem),
         name="finish",
-    )(*arrays, thin, flat, conv_out)
+    )(*arrays, thin, flat, conv_out, passed)
 
 
 def plane_peers():
@@ -1610,22 +1624,23 @@
         projected_grad.reshape(token_count, 3 * width), qkv_weight, normed, stream, mid_grad, embedded, flat_skip,
         skip_weight, flat_latent, vectors, middle_grads, hidden_bias_grad, conv_grad, resumed, here,
     )
-    skip_input_grad = skip_input_grad.reshape(row_count, tile_height, tile_width, width)
     taps = 9 * patch
     share = width // 4
     if here:
         half = width // 2
         places = [(0, 0, half, 0), (1, 0, half, 0), (1, middle_row, half, 0), (2, 0, half, 0)]
         places += [(3, 0, half, k * width) for k in range(3)] + [(4, 0, half, 0)]
-        totals = finish([place + (entry,) for place, entry in zip(places, rest[:8])], rest[8], rest[9], conv_out)
+        totals = finish([place + (entry,) for place, entry in zip(places, rest[:8])], rest[8], rest[9], conv_out, skip_input_grad)
         fc1_total, fc2_total, proj_total, qkv_total, skip_total, embed_turned, conv_grad_turned = totals[:7]
         line, fc1_line = totals[7:15], totals[15]
         output = totals[16].reshape(row_count, tile_height, tile_width, patch)
+        skip_input_grad = totals[17].reshape(skip_input.shape)
         return (
             output, skip_input_grad, embed_turned.T, line[0], skip_total, line[1], line[2], line[3], qkv_total,
             proj_total, line[4], line[5], line[6], fc1_total, fc1_line, fc2_total, line[7], conv_grad_turned.T,
         )
     output = conv_out.transpose(0, 2, 1).reshape(row_count, tile_height, tile_width, patch)
+    skip_input_grad = skip_input_grad.reshape(skip_input.shape)
     qkv_grad = jnp.concatenate([entry.reshape(-1, width) for entry in rest[:3]], axis=1)
     skip_grad, thin = [entry.reshape(-1, entry.shape[2]) for entry in rest[3:5]]
     flat = rest[5]

time: 217 us -> 216 us (level)
  no operation moved by 1% of the time
where the time goes in v2:
time: 216 us; the launch traced here: 215 us
  Pallas kernels  215 us (100%)
    pallas_call x1, Pallas kernels, attend_back(): pl.pallas_call(functools.partial(attend_back_kernel, tile_height, tile_wi...  63.3 us
    pallas_call x1, Pallas kernels, rear(): pl.pallas_call(functools.partial(rear_kernel, kinds, reduces), out_shape=...  61.3 us
    pallas_call x1, Pallas kernels, attend(): pl.pallas_call(functools.partial(attend_kernel, tile_height, tile_width),...  45.4 us
    pallas_call x1, Pallas kernels, middle(): pl.pallas_call(functools.partial(middle_kernel, paired), grid=(steps,), o...  30.1 us
    pallas_call x1, Pallas kernels, front(): pl.pallas_call(front_kernel, out_shape=[jax.ShapeDtypeStruct((token_count...  7.74 us
    pallas_call x1, Pallas kernels, finish(): pl.pallas_call(functools.partial(finish_kernel, patch, plan), out_shape=[...  6.85 us

profile of v2, /device:TPU:0, one launch (start us, length us, event | category | flops | bytes accessed | tf_op | source)
XLA Modules:
  0.0 215.5 jit_solution(6659069613068123227)
XLA Ops:
  0.7 7.7 %front.1 = (bf16[384,768]{1,0:T(8,128)(2,1)}, f32[384,768]{1,0:T(8,128)}, bf16[384,768]{1,0:T(8,128)(2,1)}, bf16[2,3,128,384]{3,2,1,0:T(8,128)(2,1)}, bf16[2,3,1...) custom-call(s32[3,32,32]{2,1,0:T(8,128)} %segment_ids.1, ...), custom_call_target="tpu_custom_call" | custom-call | tf_op jit(solution)/shard_map/front/pallas_call | solution.py:136
  8.4 45.4 %attend.1 = (bf16[2,3,128,384]{3,2,1,0:T(8,128)(2,1)}, f32[3,3,2,1,256]{4,3,2,1,0:T(1,128)}, bf16[3,2,128,384]{3,2,1,0:T(8,128)(2,1)}, bf16[3,2,128,384]{3,2,1,0...) custom-call(s32[3,2]{1,0:T(4,128)} %get-tuple-element.79.cuts, ...), custom_call_target="tpu_custom_call" | custom-call | tf_op jit(solution)/shard_map/attend/pallas_call | solution.py:912
  53.8 30.1 %middle.1 = (bf16[4,192,1536]{2,1,0:T(8,128)(2,1)}, bf16[3072,384]{1,0:T(8,128)(2,1)}, f32[4,1,768]{2,1,0:T(1,128)}, bf16[768,768]{1,0:T(8,128)(2,1)}, bf16[2,38...) custom-call(bf16[2,384,384]{2,1,0:T(8,128)(2,1)} %bitcast.22, ...), custom_call_target="tpu_custom_call" | custom-call | tf_op jit(solution)/shard_map/middle/pallas_call | solution.py:405
  83.9 63.3 %attend_back.1 = (bf16[3,128,2304]{2,1,0:T(8,128)(2,1)}, f32[768,144]{1,0:T(8,128)}, bf16[3,16,128]{2,1,0:T(8,128)(2,1)}, bf16[48,1536]{1,0:T(8,128)(2,1)}, bf16...) custom-call(s32[3,2]{1,0:T(4,128)} %get-tuple-element.79.cuts, ...), custom_call_target="tpu_custom_call" | custom-call | tf_op jit(solution)/shard_map/attend_back/pallas_call | solution.py:1218
  147.2 61.3 %rear.1 = (bf16[384,768]{1,0:T(8,128)(2,1)}, bf16[2,192,1536]{2,1,0:T(8,128)(2,1)}, bf16[2,384,384]{2,1,0:T(8,128)(2,1)}, bf16[2,384,384]{2,1,0:T(8,128)(2,1)}, ...) custom-call(bf16[384,2304]{1,0:T(8,128)(2,1)} %bitcast.17, ...), custom_call_target="tpu_custom_call" | custom-call | tf_op jit(solution)/shard_map/rear/pallas_call | solution.py:568
  208.4 6.8 %finish.1 = (f32[192,3072]{1,0:T(8,128)}, f32[768,768]{1,0:T(8,128)}, f32[192,768]{1,0:T(8,128)}, f32[192,2304]{1,0:T(8,128)}, f32[384,768]{1,0:T(8,128)}, /*ind...) custom-call(bf16[2,192,1536]{2,1,0:T(8,128)(2,1)} %get-tuple-element, ...), custom_call_target="tpu_custom_call" | custom-call | tf_op jit(solution)/shard_map/finish/pallas_call | solution.py:640

commit v3 on v2

--- a/solution.py
+++ b/solution.py
@@ -780,11 +780,13 @@
         keep(row, 0, query.at[x, row], queries.at[row, 0])
         keep(row, 1, pairs.at[x, row], here)
 
-    def forward(row):
+    def forward_x(row):
         flights[row][1].wait_recv()
         tile = held.at[row, tiles["x"]]
         send(row, 4, tile, tile, peers["y"])
         send(row, 5, tile, tile, peers["core"])
+
+    def forward_y(row):
         flights[row][2].wait_recv()
         tile = held.at[row, tiles["y"]]
         send(row, 6, tile, tile, peers["core"])
@@ -873,28 +875,36 @@
         copy.start()
         side_copies.append(copy)
 
+    begin(0)
     for copy in cot_copies:
         copy.start()
-    begin(0)
+    if row_count > 1:
+        begin(1)
+    forward_x(0)
+    for row in range(row_count):
+        for t, name in enumerate(("own", "x")):
+            fill_mask(mask.at[row, t], cuts, row, tiles[name], tile_height, tile_width)
     fill_shift(shift, tile_height, tile_width)
+    forward_y(0)
     for copy in cot_copies:
         copy.wait()
     spread_out()
-    forward(0)
-    for row in range(1, min(row_count, 3)):
-        begin(row)
     fc2_load.wait()
     activate()
-    for row in range(row_count):
-        for t, name in enumerate(("own", "x")):
-            fill_mask(mask.at[row, t], cuts, row, tiles[name], tile_height, tile_width)
+    if row_count > 1:
+        forward_x(1)
+        if row_count > 2:
+            begin(2)
+        forward_y(1)
     for row in range(row_count):
         gather_row(row)
         compute(row)
-        for later in range(1 if row == 0 else row + 2, min(row + 3, row_count)):
-            if later > 2:
-                begin(later)
-            forward(later)
+        if row + 3 < row_count:
+            begin(row + 3)
+        if row + 2 < row_count:
+            forward_x(row + 2)
+        if 0 < row < row_count - 1:
+            forward_y(row + 1)
     for row in range(row_count):
         flights[row][8].wait()
         for slot in range(3, 7):

time: 216 us -> 214 us (level)
  Pallas kernels: 215 us -> 212 us
    pallas_call x1, Pallas kernels: 45.4 us -> 42.1 us  [attend(): pl.pallas_call(functools.partial(attend_kernel, tile_height, tile_width),...]
where the time goes in v3:
time: 214 us; the launch traced here: 213 us
  Pallas kernels  212 us (99%)
    pallas_call x1, Pallas kernels, attend_back(): pl.pallas_call(functools.partial(attend_back_kernel, tile_height, tile_wi...  63.3 us
    pallas_call x1, Pallas kernels, rear(): pl.pallas_call(functools.partial(rear_kernel, kinds, reduces), out_shape=...  61.2 us
    pallas_call x1, Pallas kernels, attend(): pl.pallas_call(functools.partial(attend_kernel, tile_height, tile_width),...  42.1 us
    pallas_call x1, Pallas kernels, middle(): pl.pallas_call(functools.partial(middle_kernel, paired), grid=(steps,), o...  31.3 us
    pallas_call x1, Pallas kernels, front(): pl.pallas_call(front_kernel, out_shape=[jax.ShapeDtypeStruct((token_count...  7.74 us
    pallas_call x1, Pallas kernels, finish(): pl.pallas_call(functools.partial(finish_kernel, patch, plan), out_shape=[...  6.85 us

profile of v3, /device:TPU:0, one launch (start us, length us, event | category | flops | bytes accessed | tf_op | source)
XLA Modules:
  0.0 213.3 jit_solution(3742843876082646933)
XLA Ops:
  0.7 7.7 %front.1 = (bf16[384,768]{1,0:T(8,128)(2,1)}, f32[384,768]{1,0:T(8,128)}, bf16[384,768]{1,0:T(8,128)(2,1)}, bf16[2,3,128,384]{3,2,1,0:T(8,128)(2,1)}, bf16[2,3,1...) custom-call(s32[3,32,32]{2,1,0:T(8,128)} %segment_ids.1, ...), custom_call_target="tpu_custom_call" | custom-call | tf_op jit(solution)/shard_map/front/pallas_call | solution.py:136
  8.4 42.1 %attend.1 = (bf16[2,3,128,384]{3,2,1,0:T(8,128)(2,1)}, f32[3,3,2,1,256]{4,3,2,1,0:T(1,128)}, bf16[3,2,128,384]{3,2,1,0:T(8,128)(2,1)}, bf16[3,2,128,384]{3,2,1,0...) custom-call(s32[3,2]{1,0:T(4,128)} %get-tuple-element.79.cuts, ...), custom_call_target="tpu_custom_call" | custom-call | tf_op jit(solution)/shard_map/attend/pallas_call | solution.py:922
  50.5 31.3 %middle.1 = (bf16[4,192,1536]{2,1,0:T(8,128)(2,1)}, bf16[3072,384]{1,0:T(8,128)(2,1)}, f32[4,1,768]{2,1,0:T(1,128)}, bf16[768,768]{1,0:T(8,128)(2,1)}, bf16[2,38...) custom-call(bf16[2,384,384]{2,1,0:T(8,128)(2,1)} %bitcast.22, ...), custom_call_target="tpu_custom_call" | custom-call | tf_op jit(solution)/shard_map/middle/pallas_call | solution.py:405
  81.8 63.3 %attend_back.1 = (bf16[3,128,2304]{2,1,0:T(8,128)(2,1)}, f32[768,144]{1,0:T(8,128)}, bf16[3,16,128]{2,1,0:T(8,128)(2,1)}, bf16[48,1536]{1,0:T(8,128)(2,1)}, bf16...) custom-call(s32[3,2]{1,0:T(4,128)} %get-tuple-element.79.cuts, ...), custom_call_target="tpu_custom_call" | custom-call | tf_op jit(solution)/shard_map/attend_back/pallas_call | solution.py:1228
  145.1 61.2 %rear.1 = (bf16[384,768]{1,0:T(8,128)(2,1)}, bf16[2,192,1536]{2,1,0:T(8,128)(2,1)}, bf16[2,384,384]{2,1,0:T(8,128)(2,1)}, bf16[2,384,384]{2,1,0:T(8,128)(2,1)}, ...) custom-call(bf16[384,2304]{1,0:T(8,128)(2,1)} %bitcast.17, ...), custom_call_target="tpu_custom_call" | custom-call | tf_op jit(solution)/shard_map/rear/pallas_call | solution.py:568
  206.3 6.8 %finish.1 = (f32[192,3072]{1,0:T(8,128)}, f32[768,768]{1,0:T(8,128)}, f32[192,768]{1,0:T(8,128)}, f32[192,2304]{1,0:T(8,128)}, f32[384,768]{1,0:T(8,128)}, /*ind...) custom-call(bf16[2,192,1536]{2,1,0:T(8,128)(2,1)} %get-tuple-element, ...), custom_call_target="tpu_custom_call" | custom-call | tf_op jit(solution)/shard_map/finish/pallas_call | solution.py:640
